TPU v7x, 32 devices: a whole 2x2x4 slice. The times are simulated.
32 devices in a mesh: blk: 16 (over z, x, core), dp: 2 (over y).
Axes of the slice: x: 2, y: 2, z: 4, core: 2. Of those that a mesh axis runs over, the one named last changes fastest.
Arguments:
- inputs: bfloat16 [4096, 1024], P(('blk', 'dp')), may hold values from -6 to 6
- cotangent: bfloat16 [4096, 1024], P(('blk', 'dp')), may hold values from -2.5 to 2.5
- task_ids: int32 [4096], P(('blk', 'dp')), may hold values from 0 to 3
- group_counts: int32 [32, 8], P(('blk', 'dp')), may hold values from 1 to 16, as said below
- task_gate: float32 [4, 16], replicated, may hold values from 0.25 to 2
- w_in: bfloat16 [16, 1024, 2048], P('blk'), may hold values from -0.1875 to 0.1875
- w_out: bfloat16 [16, 2048, 1024], P('blk'), may hold values from -0.125 to 0.125
Outputs:
- input_grad: float32 [4096, 1024], P(('blk', 'dp'))
- grad_in: float32 [16, 1024, 2048], P('blk', 'dp')
- grad_out: float32 [16, 2048, 1024], P('blk', 'dp')
Inputs may be any that keep to these rules, and one draw needn't show every extreme that they name: `group_counts`: in every draw one group has all 16 slots live on every device; the others vary from device to device.
All inputs are finite; a program needn't handle non-finite values.
Results may differ from a plain program's by a relative error of at most 0.0042.
Values may be sent and summed in bfloat16 or wider, within the bound.
A program may use at most 128 MiB of HBM per device.

v0:
```python
import jax
import jax.numpy as jnp
from jax import lax
from jax.sharding import PartitionSpec as P

grad_scale = 0.0625


def shortened(array):

    def short(part):
        return part.astype(jnp.bfloat16) if part.dtype == jnp.float32 else part

    return jax.tree.map(short, array)


def shifted(array, axis, by):
    peers = lax.axis_size(axis)
    return lax.ppermute(array, axis, [(i, (i + by) % peers) for i in range(peers)])


def silu_parts(pre_act):
    sigmoid_act = jax.nn.sigmoid(pre_act)
    return (pre_act * sigmoid_act, sigmoid_act * (1.0 + pre_act * (1.0 - sigmoid_act)))


def block_grads(x_rows, cot_rows, tag_rows, first_weight, second_weight, gate_column, cut):
    task_count = gate_column.shape[0]
    matches = tag_rows[:, None] == jnp.arange(task_count, dtype=jnp.int32)[None, :]
    row_gate = jnp.sum(jnp.where(matches, gate_column[None, :], 0.0), axis=1)
    pre_act = jnp.dot(x_rows, first_weight, preferred_element_type=jnp.float32)
    act_value, act_slope = silu_parts(pre_act)
    hidden = act_value.astype(jnp.bfloat16)
    scaled_cot = (row_gate[:, None] * cot_rows.astype(jnp.float32)).astype(jnp.bfloat16)
    hidden_cot = lax.dot_general(
        scaled_cot, second_weight, (((1,), (1,)), ((), ())), preferred_element_type=jnp.float32
    )
    pre_cot = (hidden_cot * act_slope).astype(jnp.bfloat16)
    part_index, part_count = cut
    first_span = x_rows.shape[1] // part_count
    second_span = hidden.shape[1] // part_count
    left_first = lax.dynamic_slice_in_dim(x_rows, part_index * first_span, first_span, 1)
    left_second = lax.dynamic_slice_in_dim(hidden, part_index * second_span, second_span, 1)
    grad_second = lax.dot_general(
        left_second, scaled_cot, (((0,), (0,)), ((), ())), preferred_element_type=jnp.float32
    )
    grad_first = lax.dot_general(
        left_first, pre_cot, (((0,), (0,)), ((), ())), preferred_element_type=jnp.float32
    )
    return (grad_first, grad_second, pre_cot)


def expert_rows(x_rows, cot_rows, tag_rows, first_weight, second_weight, gate_column, cut):
    row_count, model_width = x_rows.shape
    hidden_width = first_weight.shape[1]
    block_rows = min(512, row_count)
    first_rows, second_rows = (model_width // cut[1], hidden_width // cut[1])
    zero_first = jnp.zeros((first_rows, hidden_width), jnp.float32)
    zero_second = jnp.zeros((second_rows, model_width), jnp.float32)
    count_blocks = row_count // block_rows

    def step_block(carry, pieces):
        grad_first, grad_second, pre_cot = block_grads(
            pieces[0], pieces[1], pieces[2], first_weight, second_weight, gate_column, cut
        )
        return ((carry[0] + grad_first, carry[1] + grad_second), pre_cot)

    blocks_in = (
        x_rows.reshape(count_blocks, block_rows, model_width),
        cot_rows.reshape(count_blocks, block_rows, model_width),
        tag_rows.reshape(count_blocks, block_rows),
    )
    sums, pre_cots = lax.scan(step_block, (zero_first, zero_second), blocks_in)
    return (sums[0], sums[1], pre_cots.reshape(row_count, hidden_width))


def run_expert(x_rows, cot_rows, tag_rows, first_weight, second_weight, gate_column):
    row_count = x_rows.shape[0]
    both_x, both_cot, both_tags = (
        lax.all_gather(x_rows, "dp", axis=0, tiled=True),
        lax.all_gather(cot_rows, "dp", axis=0, tiled=True),
        lax.all_gather(shortened(tag_rows), "dp", axis=0, tiled=True).astype(tag_rows.dtype),
    )
    half_index = lax.axis_index("dp")
    grad_first, grad_second, pre_cots = expert_rows(
        both_x,
        both_cot,
        both_tags,
        first_weight,
        second_weight,
        gate_column,
        (half_index, lax.axis_size("dp")),
    )
    own_pre = lax.dynamic_slice_in_dim(pre_cots, half_index * row_count, row_count, 0)
    row_grads = lax.dot_general(
        own_pre, first_weight, (((1,), (1,)), ((), ())), preferred_element_type=jnp.float32
    )
    return (grad_first, grad_second, row_grads)


def on_device(inputs, cotangent, task_ids, group_counts, task_gate, w_in, w_out):
    groups = group_counts.shape[1]
    model_width = inputs.shape[1]
    capacity = inputs.shape[0] // groups
    task_count = task_gate.shape[0]
    expert_count = lax.axis_size("blk")
    expert_index = lax.axis_index("blk")
    first_weight = w_in[0]
    second_weight = w_out[0]
    expert_match = jnp.arange(task_gate.shape[1], dtype=jnp.int32) == expert_index
    gate_column = jnp.sum(jnp.where(expert_match[None, :], task_gate, 0.0), axis=1)
    slot_index = jnp.arange(capacity, dtype=jnp.int32)
    live_slots = slot_index[None, :] < group_counts[0][:, None]
    seg_tags = jnp.where(live_slots, task_ids.reshape(groups, capacity), task_count)
    seg_x = inputs.reshape(groups, capacity, model_width)
    seg_cot = cotangent.reshape(groups, capacity, model_width)
    repeats = expert_count // groups
    own_group = expert_index % groups
    arrived = []
    for step_size in range(groups):
        pick = (own_group + step_size) % groups
        piece = (
            lax.dynamic_index_in_dim(seg_x, pick, 0, keepdims=False),
            lax.dynamic_index_in_dim(seg_cot, pick, 0, keepdims=False),
            lax.dynamic_index_in_dim(seg_tags, pick, 0, keepdims=False),
        )
        if step_size > 0:
            piece = shifted((piece[0], piece[1], piece[2]), "blk", step_size)
        arrived.append(piece)
    tour_x = jnp.stack([item[0] for item in arrived]).reshape(groups * capacity, model_width)
    tour_cot = jnp.stack([item[1] for item in arrived]).reshape(groups * capacity, model_width)
    tour_tags = jnp.stack([item[2] for item in arrived]).reshape(groups * capacity)
    tour_grad = jnp.zeros((groups * capacity, model_width), jnp.float32)
    grad_first = None
    grad_second = None
    for visit in range(repeats):
        part_first, part_second, row_grads = run_expert(
            tour_x, tour_cot, tour_tags, first_weight, second_weight, gate_column
        )
        grad_first = part_first if grad_first is None else grad_first + part_first
        grad_second = part_second if grad_second is None else grad_second + part_second
        tour_x, tour_cot, tour_tags, tour_grad = (
            shifted(tour_x.astype(jnp.float32), "blk", groups).astype(tour_x.dtype),
            shifted(tour_cot.astype(jnp.float32), "blk", groups).astype(tour_cot.dtype),
            shifted(tour_tags, "blk", groups),
            shifted(tour_grad + row_grads, "blk", groups),
        )
    tour_three = tour_grad.reshape(groups, capacity, model_width)
    input_home = jnp.zeros((groups, capacity, model_width), jnp.float32)
    for step_size in range(groups):
        piece = tour_three[step_size]
        if step_size > 0:
            piece = shifted(piece, "blk", -step_size)
        pick = (own_group + step_size) % groups
        input_home = lax.dynamic_update_index_in_dim(input_home, piece, pick, 0)
    first_out = (grad_first * grad_scale)[None]
    second_out = (grad_second * grad_scale)[None]
    return (input_home.reshape(groups * capacity, model_width), first_out, second_out)


def solution(mesh):
    in_specs = (
        P(("blk", "dp"), None),
        P(("blk", "dp"), None),
        P(("blk", "dp")),
        P(("blk", "dp"), None),
        P(),
        P("blk", None, None),
        P("blk", None, None),
    )
    out_specs = (P(("blk", "dp"), None), P("blk", "dp", None), P("blk", "dp", None))
    return jax.shard_map(
        on_device, mesh=mesh, in_specs=in_specs, out_specs=out_specs, check_vma=False
    )
```

profile of v0, /device:TPU:0, one launch (start us, length us, event | category | flops | bytes accessed | tf_op | source)
XLA Modules:
  0.0 159.1 jit_solution(2769633094983513002)
XLA Ops:
  2.3 2.5 %collective-permute-start.4 = (s32[16]{0:T(128)S(1)}, s32[16]{0:T(128)S(1)}, u32[]{:S(2)}, u32[]{:S(2)}) collective-permute-start(s32[16]{0:T(128)S(1)} %get-tuple-element.96), channel_id=1, source_target_pairs={{0,10},{2,12},{4,14},{6,16},{8,18},{10,20},{12,22},{14,24},{16,26}... | collective-permute-start | bytes 200 | tf_op jit(solution)/shard_map/ppermute | solution.py:19
  4.8 2.5 %collective-permute-start.5 = (s32[16]{0:T(128)S(1)}, s32[16]{0:T(128)S(1)}, u32[]{:S(2)}, u32[]{:S(2)}) collective-permute-start(s32[16]{0:T(128)S(1)} %get-tuple-element.95), channel_id=1, source_target_pairs={{0,12},{2,14},{4,16},{6,18},{8,20},{10,22},{12,24},{14,26},{16,28}... | collective-permute-start | bytes 200 | tf_op jit(solution)/shard_map/ppermute | solution.py:19
  7.3 2.1 %collective-permute-start.6 = (s32[16]{0:T(128)S(1)}, s32[16]{0:T(128)S(1)}, u32[]{:S(2)}, u32[]{:S(2)}) collective-permute-start(s32[16]{0:T(128)S(1)} %get-tuple-element.94), channel_id=1, source_target_pairs={{0,14},{2,16},{4,18},{6,20},{8,22},{10,24},{12,26},{14,28},{16,30}... | collective-permute-start | bytes 200 | tf_op jit(solution)/shard_map/ppermute | solution.py:19
  12.8 3.3 %collective-permute-start.2 = (s32[16]{0:T(128)S(1)}, s32[16]{0:T(128)S(1)}, u32[]{:S(2)}, u32[]{:S(2)}) collective-permute-start(s32[16]{0:T(128)S(1)} %get-tuple-element.98), channel_id=1, source_target_pairs={{0,6},{2,8},{4,10},{6,12},{8,14},{10,16},{12,18},{14,20},{16,22},{... | collective-permute-start | bytes 200 | tf_op jit(solution)/shard_map/ppermute | solution.py:19
  16.8 2.4 %collective-permute-start.8 = (bf16[16,1024]{1,0:T(8,128)(2,1)S(1)}, bf16[16,1024]{1,0:T(8,128)(2,1)S(1)}, u32[]{:S(2)}, u32[]{:S(2)}) collective-permute-start(bf16[16,1024]{1,0:T(8,128)(2,1)S(1)} %get-tuple-element.72), channel_id=1, source_target_pairs={{0,4},{2,6},{4,8},{6,10},{8,12},{10,14},{12,16},{14,18},{16,20},{1... | collective-permute-start | bytes 98312 | tf_op jit(solution)/shard_map/ppermute | solution.py:19
  21.6 3.0 %collective-permute-start.22 = (s32[128]{0:T(128)S(1)}, s32[128]{0:T(128)S(1)}, u32[]{:S(2)}, u32[]{:S(2)}) collective-permute-start(s32[128]{0:T(128)S(1)} %reshape.92), channel_id=1, source_target_pairs={{0,16},{2,18},{4,20},{6,22},{8,24},{10,26},{12,28},{14,30},{16,0},... | collective-permute-start | bytes 1544 | tf_op jit(solution)/shard_map/ppermute | solution.py:19
  24.7 4.2 %all-gather = s32[2,1,128]{2,1,0:T(1,128)S(1)} all-gather(s32[1,1,128]{2,1,0:T(1,128)S(1)} %reshape.98), channel_id=1, replica_groups=mesh['blk'=16,'dp'=2] {'dp'}, dimensions={0}, use_global_device_ids=true | all-gather | bytes 1536 | tf_op jit(solution)/shard_map/all_gather | solution.py:82
  29.0 4.2 %all-gather.1 = s32[2,1,128]{2,1,0:T(1,128)S(1)} all-gather(s32[1,1,128]{2,1,0:T(1,128)S(1)} %bitcast.161), channel_id=1, replica_groups=mesh['blk'=16,'dp'=2] {'dp'}, dimensions={0}, use_global_device_ids=true | all-gather | bytes 1536 | tf_op jit(solution)/shard_map/all_gather | solution.py:82
  33.6 3.0 %collective-permute-start.13 = (bf16[16,1024]{1,0:T(8,128)(2,1)S(1)}, bf16[16,1024]{1,0:T(8,128)(2,1)S(1)}, u32[]{:S(2)}, u32[]{:S(2)}) collective-permute-start(bf16[16,1024]{1,0:T(8,128)(2,1)S(1)} %get-tuple-element.67), channel_id=1, source_target_pairs={{0,14},{2,16},{4,18},{6,20},{8,22},{10,24},{12,26},{14,28},{16,30}... | collective-permute-start | bytes 98312 | tf_op jit(solution)/shard_map/ppermute | solution.py:19
  37.9 1.6 collective-permute-start.16
  41.1 1.6 collective-permute-done.14
  43.6 2.7 %collective-permute-start.20 = (bf16[16,1024]{1,0:T(8,128)(2,1)S(1)}, bf16[16,1024]{1,0:T(8,128)(2,1)S(1)}, u32[]{:S(2)}, u32[]{:S(2)}) collective-permute-start(bf16[16,1024]{1,0:T(8,128)(2,1)S(1)} %get-tuple-element.75), channel_id=1, source_target_pairs={{0,14},{2,16},{4,18},{6,20},{8,22},{10,24},{12,26},{14,28},{16,30}... | collective-permute-start | bytes 98312 | tf_op jit(solution)/shard_map/ppermute | solution.py:19
  46.3 2.5 %collective-permute-done.19 = bf16[16,1024]{1,0:T(8,128)(2,1)S(1)} collective-permute-done((bf16[16,1024]{1,0:T(8,128)(2,1)S(1)}, bf16[16,1024]{1,0:T(8,128)(2,1)S(1)}, u32[]{:S(2)}, u32[]{:S(2)}) %collective-permute-start.19) | collective-permute-done | bytes 32800 | tf_op jit(solution)/shard_map/ppermute | solution.py:19
  48.8 8.8 %all_gather.19 = bf16[256,1024]{1,0:T(8,128)(2,1)S(1)} all-gather(bf16[128,1024]{1,0:T(8,128)(2,1)S(1)} %bitcast.147), channel_id=1, replica_groups=mesh['blk'=16,'dp'=2] {'dp'}, dimensions={0}, use_global_device_ids=true | all-gather | bytes 786432 | tf_op jit(solution)/shard_map/all_gather | solution.py:81
  57.6 7.9 %all_gather.20 = bf16[256,1024]{1,0:T(8,128)(2,1)S(1)} all-gather(bf16[128,1024]{1,0:T(8,128)(2,1)S(1)} %bitcast.145), channel_id=1, replica_groups=mesh['blk'=16,'dp'=2] {'dp'}, dimensions={0}, use_global_device_ids=true | all-gather | bytes 786432 | tf_op jit(solution)/shard_map/all_gather | solution.py:80
  66.2 2.2 %collective-permute-start.24 = (bf16[128,1024]{1,0:T(8,128)(2,1)S(1)}, bf16[128,1024]{1,0:T(8,128)(2,1)S(1)}, u32[]{:S(2)}, u32[]{:S(2)}) collective-permute-start(bf16[128,1024]{1,0:T(8,128)(2,1)S(1)} %bitcast.146), channel_id=1, source_target_pairs={{0,16},{2,18},{4,20},{6,22},{8,24},{10,26},{12,28},{14,30},{16,0},... | collective-permute-start | bytes 786440 | tf_op jit(solution)/shard_map/ppermute | solution.py:19
  68.4 3.5 %add_divide_fusion.1 = (f32[256,2048]{1,0:T(8,128)S(1)}, f32[256,2048]{1,0:T(8,128)S(1)}) fusion(bf16[256,1024]{1,0:T(8,128)(2,1)S(1)} %all_gather.20, bf16[1,1024,2048]{2,1,0:T(8,128)(2,1)} %param.12), kind=kOutput, calls=%fused_computation.19 | convolution fusion | flops 1075314688 | bytes 8912896 | tf_op jit(solution)/shard_map/while/body/eval_jaxpr/dot_general | solution.py:31
  71.9 1.5 fusion.21
  75.7 1.5 fusion.4
  79.1 21.6 %collective-permute-done.24 = bf16[128,1024]{1,0:T(8,128)(2,1)S(1)} collective-permute-done((bf16[128,1024]{1,0:T(8,128)(2,1)S(1)}, bf16[128,1024]{1,0:T(8,128)(2,1)S(1)}, u32[]{:S(2)}, u32[]{:S(2)}) %collective-permute-start.24) | collective-permute-done | bytes 262176 | tf_op jit(solution)/shard_map/ppermute | solution.py:19
  100.7 8.8 %all_gather.23 = bf16[256,1024]{1,0:T(8,128)(2,1)S(1)} all-gather(bf16[128,1024]{1,0:T(8,128)(2,1)S(1)} %collective-permute-done.24), channel_id=1, replica_groups=mesh['blk'=16,'dp'=2] {'dp'}, dimensions={0}, use_global_device_ids=true | all-gather | bytes 786432 | tf_op jit(solution)/shard_map/all_gather | solution.py:80
  110.8 8.1 %all_gather.22 = bf16[256,1024]{1,0:T(8,128)(2,1)S(1)} all-gather(bf16[128,1024]{1,0:T(8,128)(2,1)S(1)} %collective-permute-done.23), channel_id=1, replica_groups=mesh['blk'=16,'dp'=2] {'dp'}, dimensions={0}, use_global_device_ids=true | all-gather | bytes 786432 | tf_op jit(solution)/shard_map/all_gather | solution.py:81
  119.0 1.5 fusion.18
  120.5 1.5 fusion.24
  122.1 2.8 %multiply_bitcast_fusion.1 = f32[1,512,2048]{2,1,0:T(8,128)} fusion(f32[512,2048]{1,0:T(8,128)S(1)} %fusion.35, bf16[256,2048]{1,0:T(8,128)(2,1)S(1)} %fusion.18, bf16[256,1024]{1,0:T(8,128)(2,1)S(1)} %all_gather.23, s32[]{:T(128)S(6)} %select_n.161), kind=kOutput, calls=%fused_computation.13 | convolution fusion | flops 538968064 | bytes 9699332 | tf_op jit(solution)/shard_map/while/body/eval_jaxpr/dot_general | solution.py:47
  124.9 2.9 %multiply_bitcast_fusion = f32[1,1024,1024]{2,1,0:T(8,128)} fusion(f32[1024,1024]{1,0:T(8,128)S(1)} %fusion.29, f32[256,2048]{1,0:T(8,128)S(1)} %get-tuple-element.104, s32[]{:T(128)S(6)} %select_n.162, f32[256,2048]{1,0:T(8,128)S(1)} %get-tuple-element.105, bf16[256,1024]{1,0:T(8,128)(2,1)S(1)} %all_gather.22, f32[256]{0:T(256)S(1)} %get-tuple-element.47), kind=kOutput, calls=%fused_computation.12 | convolution fusion | flops 540278784 | bytes 11011076 | tf_op jit(solution)/shard_map/while/body/eval_jaxpr/dot_general | solution.py:44
  127.8 17.9 %collective-permute-done.25 = f32[128,1024]{1,0:T(8,128)S(1)} collective-permute-done((f32[128,1024]{1,0:T(8,128)S(1)}, f32[128,1024]{1,0:T(8,128)S(1)}, u32[]{:S(2)}, u32[]{:S(2)}) %collective-permute-start.25) | collective-permute-done | bytes 524320 | tf_op jit(solution)/shard_map/ppermute | solution.py:19
  145.8 2.8 %collective-permute-start.27 = (f32[16,1024]{1,0:T(8,128)S(1)}, f32[16,1024]{1,0:T(8,128)S(1)}, u32[]{:S(2)}, u32[]{:S(2)}) collective-permute-start(f32[16,1024]{1,0:T(8,128)S(1)} %get-tuple-element.54), channel_id=1, source_target_pairs={{0,28},{2,30},{4,0},{6,2},{8,4},{10,6},{12,8},{14,10},{16,12},{18,... | collective-permute-start | bytes 196616 | tf_op jit(solution)/shard_map/ppermute | solution.py:19
  148.6 2.7 %collective-permute-start.30 = (f32[16,1024]{1,0:T(8,128)S(1)}, f32[16,1024]{1,0:T(8,128)S(1)}, u32[]{:S(2)}, u32[]{:S(2)}) collective-permute-start(f32[16,1024]{1,0:T(8,128)S(1)} %get-tuple-element.51), channel_id=1, source_target_pairs={{0,22},{2,24},{4,26},{6,28},{8,30},{10,0},{12,2},{14,4},{16,6},{18... | collective-permute-start | bytes 196616 | tf_op jit(solution)/shard_map/ppermute | solution.py:19
  151.4 1.6 %collective-permute-start.31 = (f32[16,1024]{1,0:T(8,128)S(1)}, f32[16,1024]{1,0:T(8,128)S(1)}, u32[]{:S(2)}, u32[]{:S(2)}) collective-permute-start(f32[16,1024]{1,0:T(8,128)S(1)} %get-tuple-element.50), channel_id=1, source_target_pairs={{0,20},{2,22},{4,24},{6,26},{8,28},{10,30},{12,0},{14,2},{16,4},{1... | collective-permute-start | bytes 196616 | tf_op jit(solution)/shard_map/ppermute | solution.py:19
  153.1 2.6 %collective-permute-done.29 = f32[16,1024]{1,0:T(8,128)S(1)} collective-permute-done((f32[16,1024]{1,0:T(8,128)S(1)}, f32[16,1024]{1,0:T(8,128)S(1)}, u32[]{:S(2)}, u32[]{:S(2)}) %collective-permute-start.29) | collective-permute-done | bytes 65568 | tf_op jit(solution)/shard_map/ppermute | solution.py:19
  156.6 1.6 %collective-permute-done.32 = f32[16,1024]{1,0:T(8,128)S(1)} collective-permute-done((f32[16,1024]{1,0:T(8,128)S(1)}, f32[16,1024]{1,0:T(8,128)S(1)}, u32[]{:S(2)}, u32[]{:S(2)}) %collective-permute-start.32) | collective-permute-done | bytes 65568 | tf_op jit(solution)/shard_map/ppermute | solution.py:19
  (91 shorter events, 20.3 us)
Async XLA Ops:
  2.3 10.5 %collective-permute-start.4 = (s32[16]{0:T(128)S(1)}, s32[16]{0:T(128)S(1)}, u32[]{:S(2)}, u32[]{:S(2)}) collective-permute-start(s32[16]{0:T(128)S(1)} %get-tuple-element.96), channel_id=1, source_target_pairs={{0,10},{2,12},{4,14},{6,16},{8,18},{10,20},{12,22},{14,24},{16,26}... | collective-permute-start | bytes 200 | tf_op jit(solution)/shard_map/ppermute | solution.py:19
  4.8 11.3 %collective-permute-start.5 = (s32[16]{0:T(128)S(1)}, s32[16]{0:T(128)S(1)}, u32[]{:S(2)}, u32[]{:S(2)}) collective-permute-start(s32[16]{0:T(128)S(1)} %get-tuple-element.95), channel_id=1, source_target_pairs={{0,12},{2,14},{4,16},{6,18},{8,20},{10,22},{12,24},{14,26},{16,28}... | collective-permute-start | bytes 200 | tf_op jit(solution)/shard_map/ppermute | solution.py:19
  7.3 9.5 %collective-permute-start.6 = (s32[16]{0:T(128)S(1)}, s32[16]{0:T(128)S(1)}, u32[]{:S(2)}, u32[]{:S(2)}) collective-permute-start(s32[16]{0:T(128)S(1)} %get-tuple-element.94), channel_id=1, source_target_pairs={{0,14},{2,16},{4,18},{6,20},{8,22},{10,24},{12,26},{14,28},{16,30}... | collective-permute-start | bytes 200 | tf_op jit(solution)/shard_map/ppermute | solution.py:19
  9.5 7.4 %collective-permute-start = (s32[16]{0:T(128)S(1)}, s32[16]{0:T(128)S(1)}, u32[]{:S(2)}, u32[]{:S(2)}) collective-permute-start(s32[16]{0:T(128)S(1)} %get-tuple-element.100), channel_id=1, source_target_pairs={{0,2},{2,4},{4,6},{6,8},{8,10},{10,12},{12,14},{14,16},{16,18},{18... | collective-permute-start | bytes 200 | tf_op jit(solution)/shard_map/ppermute | solution.py:19
  9.5 9.8 %collective-permute-start.1 = (s32[16]{0:T(128)S(1)}, s32[16]{0:T(128)S(1)}, u32[]{:S(2)}, u32[]{:S(2)}) collective-permute-start(s32[16]{0:T(128)S(1)} %get-tuple-element.99), channel_id=1, source_target_pairs={{0,4},{2,6},{4,8},{6,10},{8,12},{10,14},{12,16},{14,18},{16,20},{1... | collective-permute-start | bytes 200 | tf_op jit(solution)/shard_map/ppermute | solution.py:19
  12.8 7.6 %collective-permute-start.2 = (s32[16]{0:T(128)S(1)}, s32[16]{0:T(128)S(1)}, u32[]{:S(2)}, u32[]{:S(2)}) collective-permute-start(s32[16]{0:T(128)S(1)} %get-tuple-element.98), channel_id=1, source_target_pairs={{0,6},{2,8},{4,10},{6,12},{8,14},{10,16},{12,18},{14,20},{16,22},{... | collective-permute-start | bytes 200 | tf_op jit(solution)/shard_map/ppermute | solution.py:19
  16.2 5.4 %collective-permute-start.3 = (s32[16]{0:T(128)S(1)}, s32[16]{0:T(128)S(1)}, u32[]{:S(2)}, u32[]{:S(2)}) collective-permute-start(s32[16]{0:T(128)S(1)} %get-tuple-element.97), channel_id=1, source_target_pairs={{0,8},{2,10},{4,12},{6,14},{8,16},{10,18},{12,20},{14,22},{16,24},... | collective-permute-start | bytes 200 | tf_op jit(solution)/shard_map/ppermute | solution.py:19
  16.8 16.4 %collective-permute-start.7 = (bf16[16,1024]{1,0:T(8,128)(2,1)S(1)}, bf16[16,1024]{1,0:T(8,128)(2,1)S(1)}, u32[]{:S(2)}, u32[]{:S(2)}) collective-permute-start(bf16[16,1024]{1,0:T(8,128)(2,1)S(1)} %get-tuple-element.73), channel_id=1, source_target_pairs={{0,2},{2,4},{4,6},{6,8},{8,10},{10,12},{12,14},{14,16},{16,18},{18... | collective-permute-start | bytes 98312 | tf_op jit(solution)/shard_map/ppermute | solution.py:19
  16.8 16.8 %collective-permute-start.8 = (bf16[16,1024]{1,0:T(8,128)(2,1)S(1)}, bf16[16,1024]{1,0:T(8,128)(2,1)S(1)}, u32[]{:S(2)}, u32[]{:S(2)}) collective-permute-start(bf16[16,1024]{1,0:T(8,128)(2,1)S(1)} %get-tuple-element.72), channel_id=1, source_target_pairs={{0,4},{2,6},{4,8},{6,10},{8,12},{10,14},{12,16},{14,18},{16,20},{1... | collective-permute-start | bytes 98312 | tf_op jit(solution)/shard_map/ppermute | solution.py:19
  19.3 17.4 %collective-permute-start.9 = (bf16[16,1024]{1,0:T(8,128)(2,1)S(1)}, bf16[16,1024]{1,0:T(8,128)(2,1)S(1)}, u32[]{:S(2)}, u32[]{:S(2)}) collective-permute-start(bf16[16,1024]{1,0:T(8,128)(2,1)S(1)} %get-tuple-element.71), channel_id=1, source_target_pairs={{0,6},{2,8},{4,10},{6,12},{8,14},{10,16},{12,18},{14,20},{16,22},{... | collective-permute-start | bytes 98312 | tf_op jit(solution)/shard_map/ppermute | solution.py:19
  20.4 16.3 %collective-permute-start.10 = (bf16[16,1024]{1,0:T(8,128)(2,1)S(1)}, bf16[16,1024]{1,0:T(8,128)(2,1)S(1)}, u32[]{:S(2)}, u32[]{:S(2)}) collective-permute-start(bf16[16,1024]{1,0:T(8,128)(2,1)S(1)} %get-tuple-element.70), channel_id=1, source_target_pairs={{0,8},{2,10},{4,12},{6,14},{8,16},{10,18},{12,20},{14,22},{16,24},... | collective-permute-start | bytes 98312 | tf_op jit(solution)/shard_map/ppermute | solution.py:19
  21.6 7.3 %collective-permute-start.22 = (s32[128]{0:T(128)S(1)}, s32[128]{0:T(128)S(1)}, u32[]{:S(2)}, u32[]{:S(2)}) collective-permute-start(s32[128]{0:T(128)S(1)} %reshape.92), channel_id=1, source_target_pairs={{0,16},{2,18},{4,20},{6,22},{8,24},{10,26},{12,28},{14,30},{16,0},... | collective-permute-start | bytes 1544 | tf_op jit(solution)/shard_map/ppermute | solution.py:19
  29.0 8.9 %collective-permute-start.11 = (bf16[16,1024]{1,0:T(8,128)(2,1)S(1)}, bf16[16,1024]{1,0:T(8,128)(2,1)S(1)}, u32[]{:S(2)}, u32[]{:S(2)}) collective-permute-start(bf16[16,1024]{1,0:T(8,128)(2,1)S(1)} %get-tuple-element.69), channel_id=1, source_target_pairs={{0,10},{2,12},{4,14},{6,16},{8,18},{10,20},{12,22},{14,24},{16,26}... | collective-permute-start | bytes 98312 | tf_op jit(solution)/shard_map/ppermute | solution.py:19
  33.3 6.8 %collective-permute-start.12 = (bf16[16,1024]{1,0:T(8,128)(2,1)S(1)}, bf16[16,1024]{1,0:T(8,128)(2,1)S(1)}, u32[]{:S(2)}, u32[]{:S(2)}) collective-permute-start(bf16[16,1024]{1,0:T(8,128)(2,1)S(1)} %get-tuple-element.68), channel_id=1, source_target_pairs={{0,12},{2,14},{4,16},{6,18},{8,20},{10,22},{12,24},{14,26},{16,28}... | collective-permute-start | bytes 98312 | tf_op jit(solution)/shard_map/ppermute | solution.py:19
  33.6 6.4 %collective-permute-start.13 = (bf16[16,1024]{1,0:T(8,128)(2,1)S(1)}, bf16[16,1024]{1,0:T(8,128)(2,1)S(1)}, u32[]{:S(2)}, u32[]{:S(2)}) collective-permute-start(bf16[16,1024]{1,0:T(8,128)(2,1)S(1)} %get-tuple-element.67), channel_id=1, source_target_pairs={{0,14},{2,16},{4,18},{6,20},{8,22},{10,24},{12,26},{14,28},{16,30}... | collective-permute-start | bytes 98312 | tf_op jit(solution)/shard_map/ppermute | solution.py:19
  36.7 6.0 %collective-permute-start.14 = (bf16[16,1024]{1,0:T(8,128)(2,1)S(1)}, bf16[16,1024]{1,0:T(8,128)(2,1)S(1)}, u32[]{:S(2)}, u32[]{:S(2)}) collective-permute-start(bf16[16,1024]{1,0:T(8,128)(2,1)S(1)} %get-tuple-element.92), channel_id=1, source_target_pairs={{0,2},{2,4},{4,6},{6,8},{8,10},{10,12},{12,14},{14,16},{16,18},{18... | collective-permute-start | bytes 98312 | tf_op jit(solution)/shard_map/ppermute | solution.py:19
  36.7 6.8 %collective-permute-start.15 = (bf16[16,1024]{1,0:T(8,128)(2,1)S(1)}, bf16[16,1024]{1,0:T(8,128)(2,1)S(1)}, u32[]{:S(2)}, u32[]{:S(2)}) collective-permute-start(bf16[16,1024]{1,0:T(8,128)(2,1)S(1)} %get-tuple-element.91), channel_id=1, source_target_pairs={{0,4},{2,6},{4,8},{6,10},{8,12},{10,14},{12,16},{14,18},{16,20},{1... | collective-permute-start | bytes 98312 | tf_op jit(solution)/shard_map/ppermute | solution.py:19
  37.9 8.4 %collective-permute-start.16 = (bf16[16,1024]{1,0:T(8,128)(2,1)S(1)}, bf16[16,1024]{1,0:T(8,128)(2,1)S(1)}, u32[]{:S(2)}, u32[]{:S(2)}) collective-permute-start(bf16[16,1024]{1,0:T(8,128)(2,1)S(1)} %get-tuple-element.90), channel_id=1, source_target_pairs={{0,6},{2,8},{4,10},{6,12},{8,14},{10,16},{12,18},{14,20},{16,22},{... | collective-permute-start | bytes 98312 | tf_op jit(solution)/shard_map/ppermute | solution.py:19
  40.0 6.3 %collective-permute-start.17 = (bf16[16,1024]{1,0:T(8,128)(2,1)S(1)}, bf16[16,1024]{1,0:T(8,128)(2,1)S(1)}, u32[]{:S(2)}, u32[]{:S(2)}) collective-permute-start(bf16[16,1024]{1,0:T(8,128)(2,1)S(1)} %get-tuple-element.89), channel_id=1, source_target_pairs={{0,8},{2,10},{4,12},{6,14},{8,16},{10,18},{12,20},{14,22},{16,24},... | collective-permute-start | bytes 98312 | tf_op jit(solution)/shard_map/ppermute | solution.py:19
  40.0 6.3 %collective-permute-start.18 = (bf16[16,1024]{1,0:T(8,128)(2,1)S(1)}, bf16[16,1024]{1,0:T(8,128)(2,1)S(1)}, u32[]{:S(2)}, u32[]{:S(2)}) collective-permute-start(bf16[16,1024]{1,0:T(8,128)(2,1)S(1)} %get-tuple-element.88), channel_id=1, source_target_pairs={{0,10},{2,12},{4,14},{6,16},{8,18},{10,20},{12,22},{14,24},{16,26}... | collective-permute-start | bytes 98312 | tf_op jit(solution)/shard_map/ppermute | solution.py:19
  42.7 6.1 %collective-permute-start.19 = (bf16[16,1024]{1,0:T(8,128)(2,1)S(1)}, bf16[16,1024]{1,0:T(8,128)(2,1)S(1)}, u32[]{:S(2)}, u32[]{:S(2)}) collective-permute-start(bf16[16,1024]{1,0:T(8,128)(2,1)S(1)} %get-tuple-element.76), channel_id=1, source_target_pairs={{0,12},{2,14},{4,16},{6,18},{8,20},{10,22},{12,24},{14,26},{16,28}... | collective-permute-start | bytes 98312 | tf_op jit(solution)/shard_map/ppermute | solution.py:19
  43.6 14.0 %collective-permute-start.20 = (bf16[16,1024]{1,0:T(8,128)(2,1)S(1)}, bf16[16,1024]{1,0:T(8,128)(2,1)S(1)}, u32[]{:S(2)}, u32[]{:S(2)}) collective-permute-start(bf16[16,1024]{1,0:T(8,128)(2,1)S(1)} %get-tuple-element.75), channel_id=1, source_target_pairs={{0,14},{2,16},{4,18},{6,20},{8,22},{10,24},{12,26},{14,28},{16,30}... | collective-permute-start | bytes 98312 | tf_op jit(solution)/shard_map/ppermute | solution.py:19
  65.5 45.4 %collective-permute-start.23 = (bf16[128,1024]{1,0:T(8,128)(2,1)S(1)}, bf16[128,1024]{1,0:T(8,128)(2,1)S(1)}, u32[]{:S(2)}, u32[]{:S(2)}) collective-permute-start(bf16[128,1024]{1,0:T(8,128)(2,1)S(1)} %bitcast.148), channel_id=1, source_target_pairs={{0,16},{2,18},{4,20},{6,22},{8,24},{10,26},{12,28},{14,30},{16,0},... | collective-permute-start | bytes 786440 | tf_op jit(solution)/shard_map/ppermute | solution.py:19
  66.2 34.5 %collective-permute-start.24 = (bf16[128,1024]{1,0:T(8,128)(2,1)S(1)}, bf16[128,1024]{1,0:T(8,128)(2,1)S(1)}, u32[]{:S(2)}, u32[]{:S(2)}) collective-permute-start(bf16[128,1024]{1,0:T(8,128)(2,1)S(1)} %bitcast.146), channel_id=1, source_target_pairs={{0,16},{2,18},{4,20},{6,22},{8,24},{10,26},{12,28},{14,30},{16,0},... | collective-permute-start | bytes 786440 | tf_op jit(solution)/shard_map/ppermute | solution.py:19
  77.2 43.3 %collective-permute-start.21 = (f32[128,1024]{1,0:T(8,128)S(1)}, f32[128,1024]{1,0:T(8,128)S(1)}, u32[]{:S(2)}, u32[]{:S(2)}) collective-permute-start(f32[128,1024]{1,0:T(8,128)S(1)} %fusion.4), channel_id=1, source_target_pairs={{0,16},{2,18},{4,20},{6,22},{8,24},{10,26},{12,28},{14,30},{16,0},... | collective-permute-start | bytes 1572872 | tf_op jit(solution)/shard_map/ppermute | solution.py:19
  122.0 23.7 %collective-permute-start.25 = (f32[128,1024]{1,0:T(8,128)S(1)}, f32[128,1024]{1,0:T(8,128)S(1)}, u32[]{:S(2)}, u32[]{:S(2)}) collective-permute-start(f32[128,1024]{1,0:T(8,128)S(1)} %fusion.24), channel_id=1, source_target_pairs={{0,16},{2,18},{4,20},{6,22},{8,24},{10,26},{12,28},{14,30},{16,0},... | collective-permute-start | bytes 1572872 | tf_op jit(solution)/shard_map/ppermute | solution.py:19
  145.8 5.6 %collective-permute-start.26 = (f32[16,1024]{1,0:T(8,128)S(1)}, f32[16,1024]{1,0:T(8,128)S(1)}, u32[]{:S(2)}, u32[]{:S(2)}) collective-permute-start(f32[16,1024]{1,0:T(8,128)S(1)} %get-tuple-element.66), channel_id=1, source_target_pairs={{0,30},{2,0},{4,2},{6,4},{8,6},{10,8},{12,10},{14,12},{16,14},{18,... | collective-permute-start | bytes 196616 | tf_op jit(solution)/shard_map/ppermute | solution.py:19
  145.8 7.2 %collective-permute-start.27 = (f32[16,1024]{1,0:T(8,128)S(1)}, f32[16,1024]{1,0:T(8,128)S(1)}, u32[]{:S(2)}, u32[]{:S(2)}) collective-permute-start(f32[16,1024]{1,0:T(8,128)S(1)} %get-tuple-element.54), channel_id=1, source_target_pairs={{0,28},{2,30},{4,0},{6,2},{8,4},{10,6},{12,8},{14,10},{16,12},{18,... | collective-permute-start | bytes 196616 | tf_op jit(solution)/shard_map/ppermute | solution.py:19
  148.6 7.1 %collective-permute-start.29 = (f32[16,1024]{1,0:T(8,128)S(1)}, f32[16,1024]{1,0:T(8,128)S(1)}, u32[]{:S(2)}, u32[]{:S(2)}) collective-permute-start(f32[16,1024]{1,0:T(8,128)S(1)} %get-tuple-element.52), channel_id=1, source_target_pairs={{0,24},{2,26},{4,28},{6,30},{8,0},{10,2},{12,4},{14,6},{16,8},{18,... | collective-permute-start | bytes 196616 | tf_op jit(solution)/shard_map/ppermute | solution.py:19
  148.6 7.2 %collective-permute-start.30 = (f32[16,1024]{1,0:T(8,128)S(1)}, f32[16,1024]{1,0:T(8,128)S(1)}, u32[]{:S(2)}, u32[]{:S(2)}) collective-permute-start(f32[16,1024]{1,0:T(8,128)S(1)} %get-tuple-element.51), channel_id=1, source_target_pairs={{0,22},{2,24},{4,26},{6,28},{8,30},{10,0},{12,2},{14,4},{16,6},{18... | collective-permute-start | bytes 196616 | tf_op jit(solution)/shard_map/ppermute | solution.py:19
  151.4 5.3 %collective-permute-start.31 = (f32[16,1024]{1,0:T(8,128)S(1)}, f32[16,1024]{1,0:T(8,128)S(1)}, u32[]{:S(2)}, u32[]{:S(2)}) collective-permute-start(f32[16,1024]{1,0:T(8,128)S(1)} %get-tuple-element.50), channel_id=1, source_target_pairs={{0,20},{2,22},{4,24},{6,26},{8,28},{10,30},{12,0},{14,2},{16,4},{1... | collective-permute-start | bytes 196616 | tf_op jit(solution)/shard_map/ppermute | solution.py:19
  153.0 5.2 %collective-permute-start.32 = (f32[16,1024]{1,0:T(8,128)S(1)}, f32[16,1024]{1,0:T(8,128)S(1)}, u32[]{:S(2)}, u32[]{:S(2)}) collective-permute-start(f32[16,1024]{1,0:T(8,128)S(1)} %get-tuple-element.49), channel_id=1, source_target_pairs={{0,18},{2,20},{4,22},{6,24},{8,26},{10,28},{12,30},{14,0},{16,2},{... | collective-permute-start | bytes 196616 | tf_op jit(solution)/shard_map/ppermute | solution.py:19
  (4 other events, 13.3 us)
where the time goes:
time: 161 us; the launch traced here: 159 us
  waiting for transfers between devices  49.7 us (31%)
  blocking collectives  42 us (26%)
  starting transfers between devices  41.2 us (26%)
  matrix products  18.2 us (11%)
  local copies, waits for them, and re-layouts  5.16 us (3%)
  other arithmetic  1.62 us (1%)
    ppermute x33, waiting for transfers between devices, shifted(): lax.ppermute(array, axis, [(i, (i + by) % peers) for i in range(peers)])  49.7 us
    ppermute x33, starting transfers between devices, shifted(): lax.ppermute(array, axis, [(i, (i + by) % peers) for i in range(peers)])  41.2 us
    all_gather x2, blocking collectives, run_expert(): lax.all_gather(cot_rows, 'dp', axis=0, tiled=True)  16.9 us
    all_gather x2, blocking collectives, run_expert(): lax.all_gather(x_rows, 'dp', axis=0, tiled=True)  16.7 us
    all_gather x2, blocking collectives, run_expert(): lax.all_gather(shortened(tag_rows), 'dp', axis=0, tiled=True)  8.45 us
    dot_general x2, matrix products, block_grads(): pre_act = jnp.dot(x_rows, first_weight, preferred_element_type=jnp.float32)  4.88 us
    dot_general x2, matrix products, block_grads(): lax.dot_general(left_second, scaled_cot, (((0,), (0,)), ((), ())), prefer...  3.78 us
    dot_general x2, matrix products, block_grads(): lax.dot_general(left_first, pre_cot, (((0,), (0,)), ((), ())), preferred_...  3.52 us
  transfers between devices with their start and end apart: 33, of which 9 were waited for; matrix products, arithmetic and copies ran while one was open for 12% of the time, Pallas kernels for 0%

commit v1 on v0

v1 whole, which is shorter than its diff:
```python
import functools

import jax
import jax.numpy as jnp
from jax import lax
from jax.experimental import pallas as pl
from jax.experimental.pallas import tpu as pltpu
from jax.sharding import PartitionSpec as P

grad_scale = 0.0625
LANES = 128
MESH = pl.DeviceIdType.MESH


def exchange_kernel(
    n, peers, groups, cap, width, hidden, tasks,
    gate_ref, pay_ref, w1_hbm, w2_hbm,
    xh_out, sc_out, act_out, pc_out, home_out,
    buf, w1, w2, sc, act, pc, ret, home,
    send1, recv1, send2, recv2, send3, recv3, local_sem, out_sem,
):
    b = lax.axis_index("blk")
    h = lax.axis_index("dp")
    plane = n * cap
    half_slots = n // 2
    half_rows = half_slots * cap
    width_part = width // peers
    hidden_part = hidden // peers
    tile = 256
    tiles = hidden // tile
    part_tiles = hidden_part // tile

    def offset(i):
        odd = lax.rem(i, 2)
        return odd * ((i + 1) // 2) + (1 - odd) * lax.rem(n - i // 2, n)

    barrier = pltpu.get_barrier_semaphore()

    @pl.loop(1, n)
    def _(k):
        pl.semaphore_signal(barrier, inc=1, device_id=(lax.rem(b + k, n), h), device_id_type=MESH)

    for j in range(1, peers):
        pl.semaphore_signal(barrier, inc=1, device_id=(b, lax.rem(h + j, peers)), device_id_type=MESH)

    get_w1 = pltpu.make_async_copy(w1_hbm.at[0], w1, local_sem.at[0])
    get_w2 = pltpu.make_async_copy(w2_hbm.at[0], w2, local_sem.at[1])
    get_w1.start()
    get_w2.start()
    own = pltpu.make_async_copy(pay_ref.at[lax.rem(b, groups)], buf.at[0, pl.ds(0, cap)], local_sem.at[2])
    own.start()
    pl.semaphore_wait(barrier, n - 1 + peers - 1)

    def outgoing(i):
        target = lax.rem(b + offset(i), n)
        return pltpu.make_async_remote_copy(
            src_ref=pay_ref.at[lax.rem(target, groups)],
            dst_ref=buf.at[0, pl.ds(pl.multiple_of(i * cap, cap), cap)],
            send_sem=send1.at[i], recv_sem=recv1.at[i],
            device_id=(target, h), device_id_type=MESH,
        )

    def forward(i, j):
        rows = pl.ds(pl.multiple_of(i * cap, cap), cap)
        return pltpu.make_async_remote_copy(
            src_ref=buf.at[0, rows], dst_ref=buf.at[j, rows],
            send_sem=send2.at[j - 1, i], recv_sem=recv2.at[j - 1, i],
            device_id=(b, lax.rem(h + j, peers)), device_id_type=MESH,
        )

    def homeward(i):
        rows = pl.ds(pl.multiple_of(i * cap, cap), cap)
        target = lax.rem(b - offset(i) + n, n)
        return pltpu.make_async_remote_copy(
            src_ref=ret.at[rows], dst_ref=home.at[b],
            send_sem=send3.at[i], recv_sem=recv3.at[i],
            device_id=(target, h), device_id_type=MESH,
        )

    @pl.loop(1, n)
    def _(i):
        outgoing(i).start()

    own.wait()
    for j in range(1, peers):
        forward(0, j).start()

    def pass_on(i):
        outgoing(i).wait_recv()
        for j in range(1, peers):
            forward(i, j).start()

    @pl.loop(1, half_slots)
    def _(i):
        pass_on(i)

    get_w1.wait()
    get_w2.wait()

    def rows_forward(j, first, count, hook):
        rows = pl.ds(first, count)
        flat = pl.ds(j * plane + first, count)
        tag = buf[j, rows, pl.ds(2 * width, LANES)].astype(jnp.float32)
        gate = jnp.zeros_like(tag)
        for t in range(tasks):
            gate = gate + jnp.where(tag == float(t), gate_ref[t], 0.0)
        for c in range(width // LANES):
            cot = buf[j, rows, pl.ds(width + c * LANES, LANES)].astype(jnp.float32)
            sc[flat, pl.ds(c * LANES, LANES)] = (gate * cot).astype(jnp.bfloat16)

        def hidden_tile(q, keep):
            at = lax.rem(h * hidden_part + q * tile, hidden)
            columns = pl.ds(pl.multiple_of(at, tile), tile)
            pre = jnp.dot(
                buf[j, rows, pl.ds(0, width)], w1[:, columns], preferred_element_type=jnp.float32
            )
            sig = jax.nn.sigmoid(pre)
            if keep:
                act[flat, pl.ds(pl.multiple_of(q * tile, tile), tile)] = (pre * sig).astype(jnp.bfloat16)
            cot = lax.dot_general(
                sc[flat, :], w2[columns, :], (((1,), (1,)), ((), ())), preferred_element_type=jnp.float32
            )
            pc[flat, columns] = (cot * (sig * (1.0 + pre * (1.0 - sig)))).astype(jnp.bfloat16)
            hook(q)

        @pl.loop(0, part_tiles)
        def _(q):
            hidden_tile(q, True)

        @pl.loop(part_tiles, tiles)
        def _(q):
            hidden_tile(q, False)

    def rows_home(first, count):
        rows = pl.ds(first, count)

        @pl.loop(0, width // tile)
        def _(d):
            columns = pl.ds(pl.multiple_of(d * tile, tile), tile)
            grad = lax.dot_general(
                pc[rows, :], w1[columns, :], (((1,), (1,)), ((), ())), preferred_element_type=jnp.float32
            )
            ret[rows, columns] = grad.astype(jnp.bfloat16)

    late = n - half_slots
    per_tile = late // tiles

    def hook(q):
        for u in range(per_tile):
            pass_on(half_slots + q * per_tile + u)

    rows_forward(0, 0, half_rows, hook)
    for i in range(half_slots + tiles * per_tile, n):
        pass_on(i)
    rows_home(0, half_rows)
    own_home = pltpu.make_async_copy(ret.at[pl.ds(0, cap)], home.at[b], local_sem.at[3])
    own_home.start()

    @pl.loop(1, half_slots)
    def _(i):
        homeward(i).start()

    rows_forward(0, half_rows, plane - half_rows, lambda q: None)
    rows_home(half_rows, plane - half_rows)

    @pl.loop(half_slots, n)
    def _(i):
        homeward(i).start()

    for j in range(1, peers):
        @pl.loop(0, n)
        def _(i):
            forward(i, j).wait_recv()

        rows_forward(j, 0, plane, lambda q: None)

    x_columns = pl.ds(pl.multiple_of(h * width_part, width_part), width_part)
    stores = [
        pltpu.make_async_copy(sc, sc_out, out_sem.at[0]),
        pltpu.make_async_copy(act, act_out, out_sem.at[1]),
        pltpu.make_async_copy(pc, pc_out, out_sem.at[2]),
    ] + [
        pltpu.make_async_copy(
            buf.at[j, :, x_columns], xh_out.at[pl.ds(j * plane, plane)], out_sem.at[4 + j]
        )
        for j in range(peers)
    ]
    for store in stores:
        store.start()

    own_home.wait()

    @pl.loop(1, n)
    def _(i):
        outgoing(i).wait_send()
        homeward(i).wait_recv()

    put_home = pltpu.make_async_copy(home, home_out, out_sem.at[3])
    put_home.start()

    @pl.loop(1, n)
    def _(i):
        homeward(i).wait_send()

    for j in range(1, peers):
        @pl.loop(0, n)
        def _(i):
            forward(i, j).wait_send()

    for store in stores:
        store.wait()
    put_home.wait()


def on_device(n, peers, inputs, cotangent, task_ids, group_counts, task_gate, w_in, w_out):
    groups = group_counts.shape[1]
    width = inputs.shape[1]
    hidden = w_in.shape[2]
    cap = inputs.shape[0] // groups
    tasks = task_gate.shape[0]
    b = lax.axis_index("blk")
    match = jnp.arange(task_gate.shape[1], dtype=jnp.int32) == b
    gate_column = jnp.sum(jnp.where(match[None, :], task_gate, 0.0), axis=1)
    live = jnp.arange(cap, dtype=jnp.int32)[None, :] < group_counts[0][:, None]
    tags = jnp.where(live, task_ids.reshape(groups, cap), tasks).astype(jnp.bfloat16)
    tag_lanes = jnp.broadcast_to(tags[:, :, None], (groups, cap, LANES))
    payload = jnp.concatenate(
        [inputs.reshape(groups, cap, width), cotangent.reshape(groups, cap, width), tag_lanes], axis=2
    )
    full = 2 * width + LANES
    rows = peers * n * cap
    bf16 = jnp.bfloat16
    shape = jax.ShapeDtypeStruct
    hbm = pl.BlockSpec(memory_space=pl.ANY)
    vmem = pl.BlockSpec(memory_space=pltpu.VMEM)
    xh, sc, act, pc, home = pl.pallas_call(
        functools.partial(exchange_kernel, n, peers, groups, cap, width, hidden, tasks),
        out_shape=(
            shape((rows, width // peers), bf16),
            shape((rows, width), bf16),
            shape((rows, hidden // peers), bf16),
            shape((rows, hidden), bf16),
            shape((n, cap, width), bf16),
        ),
        in_specs=[pl.BlockSpec(memory_space=pltpu.SMEM), vmem, hbm, hbm],
        out_specs=(hbm,) * 5,
        scratch_shapes=[
            pltpu.VMEM((peers, n * cap, full), bf16),
            pltpu.VMEM((width, hidden), bf16),
            pltpu.VMEM((hidden, width), bf16),
            pltpu.VMEM((rows, width), bf16),
            pltpu.VMEM((rows, hidden // peers), bf16),
            pltpu.VMEM((rows, hidden), bf16),
            pltpu.VMEM((n * cap, width), bf16),
            pltpu.VMEM((n, cap, width), bf16),
            pltpu.SemaphoreType.DMA((n,)),
            pltpu.SemaphoreType.DMA((n,)),
            pltpu.SemaphoreType.DMA((peers - 1, n)),
            pltpu.SemaphoreType.DMA((peers - 1, n)),
            pltpu.SemaphoreType.DMA((n,)),
            pltpu.SemaphoreType.DMA((n,)),
            pltpu.SemaphoreType.DMA((4,)),
            pltpu.SemaphoreType.DMA((4 + peers,)),
        ],
        compiler_params=pltpu.CompilerParams(collective_id=0, has_side_effects=True),
    )(gate_column, payload, w_in, w_out)
    turned = (((0,), (0,)), ((), ()))
    first = lax.dot_general(xh, pc, turned, preferred_element_type=jnp.float32) * grad_scale
    second = lax.dot_general(act, sc, turned, preferred_element_type=jnp.float32) * grad_scale
    repeats = n // groups
    input_grad = jnp.sum(home.reshape(repeats, groups * cap, width).astype(jnp.float32), axis=0)
    return input_grad, first[None], second[None]


def solution(mesh):
    in_specs = (
        P(("blk", "dp"), None),
        P(("blk", "dp"), None),
        P(("blk", "dp")),
        P(("blk", "dp"), None),
        P(),
        P("blk", None, None),
        P("blk", None, None),
    )
    out_specs = (P(("blk", "dp"), None), P("blk", "dp", None), P("blk", "dp", None))
    body = functools.partial(on_device, mesh.shape["blk"], mesh.shape["dp"])
    return jax.shard_map(body, mesh=mesh, in_specs=in_specs, out_specs=out_specs, check_vma=False)
```

time: 161 us -> 64.4 us (0.40)
  waiting for transfers between devices: 49.7 us -> 0 us
  Pallas kernels: 0 us -> 47.6 us
  blocking collectives: 42 us -> 0 us
  starting transfers between devices: 41.2 us -> 0 us
  matrix products: 18.2 us -> 8.37 us
  other arithmetic: 1.62 us -> 6.04 us
  local copies, waits for them, and re-layouts: 5.16 us -> 0.82 us
    ppermute x33 -> x0, waiting for transfers between devices: 49.7 us -> none  [shifted(): lax.ppermute(array, axis, [(i, (i + by) % peers) for i in range(peers)])]
    pallas_call x0 -> x1, Pallas kernels: none -> 47.6 us  [on_device(): pl.pallas_call(functools.partial(exchange_kernel, n, peers, groups, cap,...]
    all_gather x6 -> x0, blocking collectives: 42 us -> none  [the longest x2 16.9 us: run_expert(): lax.all_gather(cot_rows, 'dp', axis=0, tiled=True)]
    ppermute x33 -> x0, starting transfers between devices: 41.2 us -> none  [shifted(): lax.ppermute(array, axis, [(i, (i + by) % peers) for i in range(peers)])]
    dot_general x10 -> x2, matrix products: 18.2 us -> 8.37 us  [the longest x1 5.06 us: on_device(): lax.dot_general(xh, pc, turned, preferred_element_type=jnp.float32)]
    reduce_sum x2, other arithmetic: 0.88 us -> 3.42 us  [the longest x1 2.11 us: on_device(): jnp.sum(home.reshape(repeats, groups * cap, width).astype(jnp.float32), a...]
    unnamed x19 -> x4, local copies, waits for them, and re-layouts: 2.34 us -> 0.01 us
    concatenate x0 -> x1, other arithmetic: none -> 1.88 us  [on_device(): jnp.concatenate([inputs.reshape(groups, cap, width), cotangent.reshape(gr...]
  transfers between devices with their start and end apart: 33 -> 0, of which waited for: 9 -> 0; matrix products, arithmetic and copies ran while one was open for 12% -> 0% of each run, Pallas kernels for 0% -> 0%
where the time goes in v1:
time: 64.4 us; the launch traced here: 63.5 us
  Pallas kernels  47.6 us (74%)
  matrix products  8.37 us (13%)
  other arithmetic  6.04 us (9%)
  local copies, waits for them, and re-layouts  0.82 us (1%)
  between operations  0.68 us (1%)
    pallas_call x1, Pallas kernels, on_device(): pl.pallas_call(functools.partial(exchange_kernel, n, peers, groups, cap,...  47.6 us
    dot_general x1, matrix products, on_device(): lax.dot_general(xh, pc, turned, preferred_element_type=jnp.float32)  5.06 us
    dot_general x1, matrix products, on_device(): lax.dot_general(act, sc, turned, preferred_element_type=jnp.float32)  3.31 us
    reduce_sum x1, other arithmetic, on_device(): jnp.sum(home.reshape(repeats, groups * cap, width).astype(jnp.float32), a...  2.11 us
    concatenate x1, other arithmetic, on_device(): jnp.concatenate([inputs.reshape(groups, cap, width), cotangent.reshape(gr...  1.88 us
    reduce_sum x1, other arithmetic, on_device(): gate_column = jnp.sum(jnp.where(match[None, :], task_gate, 0.0), axis=1)  1.31 us

profile of v1, /device:TPU:0, one launch (start us, length us, event | category | flops | bytes accessed | tf_op | source)
XLA Modules:
  0.0 63.5 jit_solution(4806897752771310210)
XLA Ops:
  0.6 1.3 %select_reduce_fusion.gate_ref = f32[4]{0:T(128)} fusion(f32[4,16]{1,0:T(4,128)} %param.11, pred[16]{0:T(512)(128)(4,1)S(1)} %iota_compare_fusion.1), kind=kLoop, calls=%fused_computation.6 | loop fusion | flops 124 | bytes 288 | tf_op jit(solution)/shard_map/reduce_sum | solution.py:223
  2.0 0.7 %reshape.54 = s32[8,16]{1,0:T(8,128)S(1)} reshape(s32[128]{0:T(128)} %param.9) | data formatting | bytes 1024 | tf_op jit(solution)/shard_map/reshape | solution.py:225
  2.7 0.7 %select_convert_fusion = bf16[8,16]{1,0:T(8,128)(2,1)S(1)} fusion(s32[8,16]{1,0:T(8,128)S(1)} %reshape.54, s32[8]{0:T(128)} %bitcast.18), kind=kLoop, calls=%fused_computation.4 | loop fusion | flops 384 | bytes 800 | tf_op jit(solution)/shard_map/convert_element_type | solution.py:225
  3.4 0.1 broadcast_in_dim.33
  3.5 1.9 %pad_maximum_fusion.pay_ref = bf16[8,16,2176]{2,1,0:T(8,128)(2,1)} fusion(bf16[8,16,128]{2,1,0:T(8,128)(2,1)S(1)} %broadcast_in_dim.33, bf16[8,16,1024]{2,1,0:T(8,128)(2,1)} %bitcast.16, bf16[8,16,1024]{2,1,0:T(8,128)(2,1)} %bitcast.17), kind=kLoop, calls=%fused_computation.3 | loop fusion | flops 1671168 | bytes 1114112 | tf_op jit(solution)/shard_map/concatenate | solution.py:227
  5.4 47.6 %shard_map.94 = (bf16[512,512]{1,0:T(8,128)(2,1)}, bf16[512,1024]{1,0:T(8,128)(2,1)}, bf16[512,1024]{1,0:T(8,128)(2,1)}, bf16[512,2048]{1,0:T(8,128)(2,1)}, bf16[16,16,1024]{2,1,0:T(8,128)(2,1)}) custom-call(f32[4]{0:T(128)} %select_reduce_fusion.gate_ref, bf16[8,16,2176]{2,1,0:T(8,128)(2,1)} %pad_maximum_fusion.pay_ref, bf16[1,1024,2048]{2,1,0:T(8,128)(2,1)} %w1_hbm.1, ...), custom_call_target="tpu_custom_call" | custom-call | tf_op jit(solution)/shard_map/pallas_call | solution.py:236
  53.0 0.0 copy-start
  53.0 0.0 copy-start.1
  53.0 2.1 %convert_reduce_fusion = f32[128,1024]{1,0:T(8,128)} fusion(bf16[2,128,1024]{2,1,0:T(8,128)(2,1)} %bitcast.15), kind=kLoop, calls=%fused_computation.2 | loop fusion | flops 393216 | bytes 1048576 | tf_op jit(solution)/shard_map/reduce_sum | solution.py:271
  55.1 5.1 %multiply_bitcast_fusion.1 = f32[1,512,2048]{2,1,0:T(8,128)} fusion(bf16[512,512]{1,0:T(8,128)(2,1)} %get-tuple-element.9, bf16[512,2048]{1,0:T(8,128)(2,1)} %get-tuple-element.10), kind=kOutput, calls=%fused_computation.1 | convolution fusion | flops 1074790400 | bytes 6815744 | tf_op jit(solution)/shard_map/dot_general | solution.py:268
  60.2 0.0 copy-done
  60.2 0.0 copy-done.1
  60.2 3.3 %multiply_bitcast_fusion = f32[1,1024,1024]{2,1,0:T(8,128)} fusion(bf16[512,1024]{1,0:T(8,128)(2,1)S(1)} %copy-done.1, bf16[512,1024]{1,0:T(8,128)(2,1)S(1)} %copy-done), kind=kOutput, calls=%fused_computation | convolution fusion | flops 1074790400 | bytes 6291456 | tf_op jit(solution)/shard_map/dot_general | solution.py:269
  (1 shorter events, 0.0 us)
Async XLA Ops:
  53.0 7.2 %copy-start = (bf16[512,1024]{1,0:T(8,128)(2,1)S(1)}, bf16[512,1024]{1,0:T(8,128)(2,1)}, u32[]{:S(2)}) copy-start(bf16[512,1024]{1,0:T(8,128)(2,1)} %get-tuple-element.12) | copy-start | bytes 3145732
  53.0 7.2 %copy-start.1 = (bf16[512,1024]{1,0:T(8,128)(2,1)S(1)}, bf16[512,1024]{1,0:T(8,128)(2,1)}, u32[]{:S(2)}) copy-start(bf16[512,1024]{1,0:T(8,128)(2,1)} %get-tuple-element.11) | copy-start | bytes 3145732

commit v2 on v1

v2 whole, which is shorter than its diff:
```python
import functools

import jax
import jax.numpy as jnp
from jax import lax
from jax.experimental import pallas as pl
from jax.experimental.pallas import tpu as pltpu
from jax.sharding import PartitionSpec as P

grad_scale = 0.0625
VMEM_BYTES = 40 * 1024 * 1024
MESH = pl.DeviceIdType.MESH


def exchange_kernel(
    n, peers, groups, cap, width, hidden, tasks,
    counts_ref, gate_ref, ids_ref, x_hbm, cot_hbm, w1_hbm, w2_hbm,
    xh, sc, act, pc, home,
    pay, tag, buf, tags, w1, w2, ret,
    send1, recv1, send2, recv2, send3, recv3, tag_send, tag_recv, tag_pass, tag_take, local_sem,
):
    b = lax.axis_index("blk")
    h = lax.axis_index("dp")
    plane = n * cap
    half, quarter = n // 2, n // 4
    width_part = width // peers
    hidden_part = hidden // peers
    tile = 256
    tiles = hidden // tile
    part_tiles = hidden_part // tile
    side, place = b // half, lax.rem(b, half)
    step, spot = place // quarter, lax.rem(place, quarter)
    own_group = lax.rem(b, groups)

    def near_target(i):
        return side * half + lax.rem(place - i + half, half)

    def far_target(i):
        return (1 - side) * half + (i // quarter) * quarter + lax.rem(spot - lax.rem(i, quarter) + quarter, quarter)

    def far_slot(i):
        return half + lax.rem(step + side + 1, 2) * quarter + lax.rem(i, quarter)

    def near_source(i):
        return side * half + lax.rem(place + i, half)

    def far_source(i):
        far = i - half
        ring = far // quarter
        return (1 - side) * half + lax.rem(side + ring, 2) * quarter + lax.rem(spot + lax.rem(far, quarter), quarter)

    def slot_rows(i):
        return pl.ds(pl.multiple_of(i * cap, cap), cap)

    barrier = pltpu.get_barrier_semaphore()

    @pl.loop(1, n)
    def _(k):
        pl.semaphore_signal(barrier, inc=1, device_id=(lax.rem(b + k, n), h), device_id_type=MESH)

    for j in range(1, peers):
        pl.semaphore_signal(barrier, inc=1, device_id=(b, lax.rem(h + j, peers)), device_id_type=MESH)

    get_x = pltpu.make_async_copy(x_hbm, pay.at[:, :, pl.ds(0, width)], local_sem.at[0])
    get_cot = pltpu.make_async_copy(cot_hbm, pay.at[:, :, pl.ds(width, width)], local_sem.at[1])
    get_x.start()
    get_cot.start()

    lane = lax.broadcasted_iota(jnp.int32, tag.shape, 1)
    limit = jnp.zeros(tag.shape, jnp.int32)
    for g in range(groups):
        limit = jnp.where(lane // cap == g, counts_ref[0, g] + g * cap, limit)
    tag[...] = jnp.where(lane < limit, ids_ref[...], tasks).astype(jnp.float32)
    tags[0, 0] = tag[...]

    get_x.wait()
    get_cot.wait()
    own = pltpu.make_async_copy(pay.at[own_group], buf.at[0, pl.ds(0, cap)], local_sem.at[2])
    own.start()
    get_w1 = pltpu.make_async_copy(w1_hbm.at[0], w1, local_sem.at[3])
    get_w2 = pltpu.make_async_copy(w2_hbm.at[0], w2, local_sem.at[4])
    get_w1.start()
    get_w2.start()
    pl.semaphore_wait(barrier, n - 1 + peers - 1)

    def block_out(target, at, slot):
        return pltpu.make_async_remote_copy(
            src_ref=pay.at[lax.rem(target, groups)], dst_ref=buf.at[0, slot_rows(slot)],
            send_sem=send1.at[at], recv_sem=recv1.at[slot],
            device_id=(target, h), device_id_type=MESH,
        )

    def tag_out(target, at, slot):
        return pltpu.make_async_remote_copy(
            src_ref=tag, dst_ref=tags.at[0, slot],
            send_sem=tag_send.at[at], recv_sem=tag_recv.at[slot],
            device_id=(target, h), device_id_type=MESH,
        )

    def tags_on(j):
        return pltpu.make_async_remote_copy(
            src_ref=tags.at[0], dst_ref=tags.at[j],
            send_sem=tag_pass.at[j - 1], recv_sem=tag_take.at[j - 1],
            device_id=(b, lax.rem(h + j, peers)), device_id_type=MESH,
        )

    def forward(i, j):
        return pltpu.make_async_remote_copy(
            src_ref=buf.at[0, slot_rows(i)], dst_ref=buf.at[j, slot_rows(i)],
            send_sem=send2.at[j - 1, i], recv_sem=recv2.at[j - 1, i],
            device_id=(b, lax.rem(h + j, peers)), device_id_type=MESH,
        )

    def homeward(i, target):
        return pltpu.make_async_remote_copy(
            src_ref=ret.at[slot_rows(i)], dst_ref=home.at[b],
            send_sem=send3.at[i], recv_sem=recv3.at[b],
            device_id=(target, h), device_id_type=MESH,
        )

    def home_from(source):
        return pltpu.make_async_remote_copy(
            src_ref=ret.at[slot_rows(0)], dst_ref=home.at[source],
            send_sem=send3.at[0], recv_sem=recv3.at[source],
            device_id=(source, h), device_id_type=MESH,
        )

    @pl.loop(1, half)
    def _(i):
        tag_out(near_target(i), i, i).start()
        block_out(near_target(i), i, i).start()

    @pl.loop(0, half)
    def _(i):
        tag_out(far_target(i), half + i, far_slot(i)).start()
        block_out(far_target(i), half + i, far_slot(i)).start()

    own.wait()
    for j in range(1, peers):
        forward(0, j).start()

    def pass_on(i):
        block_out(near_target(0), i, i).wait_recv()
        for j in range(1, peers):
            forward(i, j).start()

    @pl.loop(1, half)
    def _(i):
        pass_on(i)

    @pl.loop(1, n)
    def _(i):
        tag_out(near_target(0), i, i).wait_recv()

    for j in range(1, peers):
        tags_on(j).start()
    get_w1.wait()
    get_w2.wait()

    def rows_forward(j, slot, count, hook):
        first, total = slot * cap, count * cap
        rows = pl.ds(first, total)
        flat = pl.ds(j * plane + first, total)
        known = tags[j, pl.ds(slot, count)]
        gates = jnp.zeros_like(known)
        for t in range(tasks):
            gates = gates + jnp.where(known == float(t), gate_ref[t, b], 0.0)
        spread = jnp.broadcast_to(gates, (count, cap, groups * cap))
        lanes = lax.broadcasted_iota(jnp.int32, spread.shape, 2)
        places = lax.broadcasted_iota(jnp.int32, spread.shape, 1) + own_group * cap
        gate = jnp.sum(jnp.where(lanes == places, spread, 0.0), axis=2, keepdims=True).reshape(total, 1)
        cot_rows = buf[j, rows, pl.ds(width, width)].astype(jnp.float32)
        sc[flat, :] = (gate * cot_rows).astype(jnp.bfloat16)
        xh[flat, :] = buf[j, rows, pl.ds(pl.multiple_of(h * width_part, width_part), width_part)]

        def hidden_tile(q, keep):
            at = lax.rem(h * hidden_part + q * tile, hidden)
            columns = pl.ds(pl.multiple_of(at, tile), tile)
            pre = jnp.dot(
                buf[j, rows, pl.ds(0, width)], w1[:, columns], preferred_element_type=jnp.float32
            )
            sig = jax.nn.sigmoid(pre)
            if keep:
                act[flat, pl.ds(pl.multiple_of(q * tile, tile), tile)] = (pre * sig).astype(jnp.bfloat16)
            cot = lax.dot_general(
                sc[flat, :], w2[columns, :], (((1,), (1,)), ((), ())), preferred_element_type=jnp.float32
            )
            pc[flat, columns] = (cot * (sig * (1.0 + pre * (1.0 - sig)))).astype(jnp.bfloat16)
            hook(q)

        @pl.loop(0, part_tiles)
        def _(q):
            hidden_tile(q, True)

        @pl.loop(part_tiles, tiles)
        def _(q):
            hidden_tile(q, False)

    def rows_home(slot, count):
        rows = pl.ds(slot * cap, count * cap)

        @pl.loop(0, width // tile)
        def _(d):
            columns = pl.ds(pl.multiple_of(d * tile, tile), tile)
            grad = lax.dot_general(
                pc[rows, :], w1[columns, :], (((1,), (1,)), ((), ())), preferred_element_type=jnp.float32
            )
            ret[rows, columns] = grad.astype(jnp.bfloat16)

    rows_forward(0, 0, half, lambda q: None)
    rows_home(0, half)
    own_home = pltpu.make_async_copy(ret.at[pl.ds(0, cap)], home.at[b], local_sem.at[5])
    own_home.start()

    @pl.loop(1, half)
    def _(i):
        homeward(i, near_source(i)).start()

    for first in (half, half + quarter):
        @pl.loop(first, first + quarter)
        def _(i):
            pass_on(i)

        rows_forward(0, first, quarter, lambda q: None)
        rows_home(first, quarter)

        @pl.loop(first, first + quarter)
        def _(i):
            homeward(i, far_source(i)).start()

    for j in range(1, peers):
        tags_on(j).wait_recv()

        @pl.loop(0, n)
        def _(i):
            forward(i, j).wait_recv()

        rows_forward(j, 0, n, lambda q: None)

    own_home.wait()

    @pl.loop(1, n)
    def _(i):
        block_out(near_target(0), i, i).wait_send()
        tag_out(near_target(0), i, i).wait_send()
        homeward(i, b).wait_send()

    for j in range(1, peers):
        tags_on(j).wait_send()

        @pl.loop(0, n)
        def _(i):
            forward(i, j).wait_send()

    @pl.loop(1, n)
    def _(k):
        home_from(lax.rem(b + k, n)).wait_recv()


def on_device(n, peers, inputs, cotangent, task_ids, group_counts, task_gate, w_in, w_out):
    groups = group_counts.shape[1]
    slots, width = inputs.shape
    hidden = w_in.shape[2]
    cap = slots // groups
    tasks = task_gate.shape[0]
    rows = peers * n * cap
    bf16 = jnp.bfloat16
    hbm = pl.BlockSpec(memory_space=pltpu.HBM)
    smem = pl.BlockSpec(memory_space=pltpu.SMEM)
    vmem = pl.BlockSpec(memory_space=pltpu.VMEM)
    dma = pltpu.SemaphoreType.DMA
    xh, sc, act, pc, home = pl.pallas_call(
        functools.partial(exchange_kernel, n, peers, groups, cap, width, hidden, tasks),
        out_shape=(
            pltpu.VMEM((rows, width // peers), bf16),
            pltpu.VMEM((rows, width), bf16),
            pltpu.VMEM((rows, hidden // peers), bf16),
            pltpu.VMEM((rows, hidden), bf16),
            pltpu.VMEM((n, cap, width), bf16),
        ),
        in_specs=[smem, smem, vmem, hbm, hbm, hbm, hbm],
        out_specs=(vmem,) * 5,
        scratch_shapes=[
            pltpu.VMEM((groups, cap, 2 * width), bf16),
            pltpu.VMEM((1, slots), jnp.float32),
            pltpu.VMEM((peers, n * cap, 2 * width), bf16),
            pltpu.VMEM((peers, n, 1, slots), jnp.float32),
            pltpu.VMEM((width, hidden), bf16),
            pltpu.VMEM((hidden, width), bf16),
            pltpu.VMEM((n * cap, width), bf16),
            dma((n,)), dma((n,)), dma((peers - 1, n)), dma((peers - 1, n)), dma((n,)), dma((n,)),
            dma((n,)), dma((n,)), dma((peers - 1,)), dma((peers - 1,)), dma((6,)),
        ],
        compiler_params=pltpu.CompilerParams(
            collective_id=0, has_side_effects=True, vmem_limit_bytes=VMEM_BYTES
        ),
    )(
        group_counts, task_gate, task_ids.reshape(1, slots),
        *(
            pltpu.with_memory_space_constraint(array, pltpu.HBM)
            for array in (inputs.reshape(groups, cap, width), cotangent.reshape(groups, cap, width), w_in, w_out)
        ),
    )
    turned = (((0,), (0,)), ((), ()))
    first = lax.dot_general(xh, pc, turned, preferred_element_type=jnp.float32) * grad_scale
    second = lax.dot_general(act, sc, turned, preferred_element_type=jnp.float32) * grad_scale
    repeats = n // groups
    input_grad = jnp.sum(home.reshape(repeats, groups * cap, width).astype(jnp.float32), axis=0)
    return input_grad, first[None], second[None]


def solution(mesh):
    in_specs = (
        P(("blk", "dp"), None),
        P(("blk", "dp"), None),
        P(("blk", "dp")),
        P(("blk", "dp"), None),
        P(),
        P("blk", None, None),
        P("blk", None, None),
    )
    out_specs = (P(("blk", "dp"), None), P("blk", "dp", None), P("blk", "dp", None))
    body = functools.partial(on_device, mesh.shape["blk"], mesh.shape["dp"])
    return jax.shard_map(body, mesh=mesh, in_specs=in_specs, out_specs=out_specs, check_vma=False)
```

time: 64.4 us -> 63 us (0.978); the launches traced: 63.5 us -> 62.8 us
  other arithmetic: 6.04 us -> 0.89 us
  Pallas kernels: 47.6 us -> 52.7 us
  matrix products: 8.37 us -> 6.6 us
  local copies, waits for them, and re-layouts: 0.82 us -> 1.98 us
    pallas_call x1, Pallas kernels: 47.6 us -> 52.7 us  [on_device(): pl.pallas_call(functools.partial(exchange_kernel, n, peers, groups, cap,...]
    unnamed x4 -> x6, local copies, waits for them, and re-layouts: 0.01 us -> 1.98 us
    concatenate x1 -> x0, other arithmetic: 1.88 us -> none  [on_device(): jnp.concatenate([inputs.reshape(groups, cap, width), cotangent.reshape(gr...]
    dot_general x1, matrix products: 5.06 us -> 3.3 us  [on_device(): lax.dot_general(xh, pc, turned, preferred_element_type=jnp.float32)]
    reduce_sum x1 -> x0, other arithmetic: 1.31 us -> none  [on_device(): gate_column = jnp.sum(jnp.where(match[None, :], task_gate, 0.0), axis=1)]
    reduce_sum x1, other arithmetic: 2.11 us -> 0.89 us  [on_device(): jnp.sum(home.reshape(repeats, groups * cap, width).astype(jnp.float32), a...]
    convert_element_type x1 -> x0, other arithmetic: 0.73 us -> none  [on_device(): jnp.where(live, task_ids.reshape(groups, cap), tasks).astype(jnp.bfloat16)]
    reshape x1 -> x0, local copies, waits for them, and re-layouts: 0.73 us -> none  [on_device(): task_ids.reshape(groups, cap)]
where the time goes in v2:
time: 63 us; the launch traced here: 62.8 us
  Pallas kernels  52.7 us (84%)
  matrix products  6.6 us (10%)
  local copies, waits for them, and re-layouts  1.98 us (3%)
  other arithmetic  0.89 us (1%)
  between operations  0.65 us (1%)
    pallas_call x1, Pallas kernels, on_device(): pl.pallas_call(functools.partial(exchange_kernel, n, peers, groups, cap,...  52.7 us
    dot_general x1, matrix products, on_device(): lax.dot_general(act, sc, turned, preferred_element_type=jnp.float32)  3.31 us
    dot_general x1, matrix products, on_device(): lax.dot_general(xh, pc, turned, preferred_element_type=jnp.float32)  3.3 us
    unnamed x6, local copies, waits for them, and re-layouts  1.98 us

profile of v2, /device:TPU:0, one launch (start us, length us, event | category | flops | bytes accessed | tf_op | source)
XLA Modules:
  0.0 62.8 jit_solution(10142134013203612174)
XLA Ops:
  0.6 0.0 copy-start
  0.6 0.7 %copy-done = f32[4,16]{1,0:T(4,128)S(1)} copy-done((f32[4,16]{1,0:T(4,128)S(1)}, f32[4,16]{1,0:T(4,128)}, u32[]{:S(2)}) %copy-start) | copy-done | bytes 280
  1.3 0.0 copy-start.1
  1.3 0.7 %copy-done.1 = s32[1,8]{1,0:T(1,128)S(1)} copy-done((s32[1,8]{1,0:T(1,128)S(1)}, s32[1,8]{1,0:T(1,128)}, u32[]{:S(2)}) %copy-start.1) | copy-done | bytes 56
  2.0 0.0 copy-start.2
  2.0 0.7 %copy-done.2 = s32[128]{0:T(128)S(1)} copy-done((s32[128]{0:T(128)S(1)}, s32[128]{0:T(128)}, u32[]{:S(2)}) %copy-start.2) | copy-done | bytes 536
  2.6 52.7 %shard_map.94 = (bf16[512,512]{1,0:T(8,128)(2,1)S(1)}, bf16[512,1024]{1,0:T(8,128)(2,1)S(1)}, bf16[512,1024]{1,0:T(8,128)(2,1)S(1)}, bf16[512,2048]{1,0:T(8,128)(2,1)S(1)}, bf16[16,16,1024]{2,1,0:T(8,128)(2,1)S(1)}) custom-call(s32[1,8]{1,0:T(1,128)S(1)} %copy-done.1, f32[4,16]{1,0:T(4,128)S(1)} %copy-done, s32[1,128]{1,0:T(1,128)S(1)} %bitcast.16, ...), custom_call_target="tpu_custom_call" | custom-call | tf_op jit(solution)/shard_map/pallas_call | solution.py:272
  55.3 0.9 %convert_reduce_fusion = f32[128,1024]{1,0:T(8,128)} fusion(bf16[2,128,1024]{2,1,0:T(8,128)(2,1)S(1)} %bitcast.15), kind=kLoop, calls=%fused_computation.2 | loop fusion | flops 393216 | bytes 1048576 | tf_op jit(solution)/shard_map/reduce_sum | solution.py:308
  56.2 3.3 %multiply_bitcast_fusion.1 = f32[1,512,2048]{2,1,0:T(8,128)} fusion(bf16[512,512]{1,0:T(8,128)(2,1)S(1)} %get-tuple-element.9, bf16[512,2048]{1,0:T(8,128)(2,1)S(1)} %get-tuple-element.10), kind=kOutput, calls=%fused_computation.1 | convolution fusion | flops 1074790400 | bytes 6815744 | tf_op jit(solution)/shard_map/dot_general | solution.py:305
  59.5 3.3 %multiply_bitcast_fusion = f32[1,1024,1024]{2,1,0:T(8,128)} fusion(bf16[512,1024]{1,0:T(8,128)(2,1)S(1)} %get-tuple-element.11, bf16[512,1024]{1,0:T(8,128)(2,1)S(1)} %get-tuple-element.12), kind=kOutput, calls=%fused_computation | convolution fusion | flops 1074790400 | bytes 6291456 | tf_op jit(solution)/shard_map/dot_general | solution.py:306
Async XLA Ops:
  0.6 0.7 %copy-start = (f32[4,16]{1,0:T(4,128)S(1)}, f32[4,16]{1,0:T(4,128)}, u32[]{:S(2)}) copy-start(f32[4,16]{1,0:T(4,128)} %gate_ref.1) | copy-start | bytes 772
  1.3 0.7 %copy-start.1 = (s32[1,8]{1,0:T(1,128)S(1)}, s32[1,8]{1,0:T(1,128)}, u32[]{:S(2)}) copy-start(s32[1,8]{1,0:T(1,128)} %counts_ref.1) | copy-start | bytes 100
  2.0 0.7 %copy-start.2 = (s32[128]{0:T(128)S(1)}, s32[128]{0:T(128)}, u32[]{:S(2)}) copy-start(s32[128]{0:T(128)} %param.9) | copy-start | bytes 1540

commit v3 on v2

--- a/solution.py
+++ b/solution.py
@@ -14,10 +14,10 @@
 
 def exchange_kernel(
     n, peers, groups, cap, width, hidden, tasks,
-    counts_ref, gate_ref, ids_ref, x_hbm, cot_hbm, w1_hbm, w2_hbm,
+    counts_hbm, gate_hbm, ids_hbm, x_hbm, cot_hbm, w1_hbm, w2_hbm,
     xh, sc, act, pc, home,
-    pay, tag, buf, tags, w1, w2, ret,
-    send1, recv1, send2, recv2, send3, recv3, tag_send, tag_recv, tag_pass, tag_take, local_sem,
+    counts_ref, gate_ref, ids_ref, cots, tag, pay, buf, w1, w2, ret,
+    send1, recv1, send2, recv2, send3, recv3, local_sem,
 ):
     b = lax.axis_index("blk")
     h = lax.axis_index("dp")
@@ -30,24 +30,32 @@
     part_tiles = hidden_part // tile
     side, place = b // half, lax.rem(b, half)
     step, spot = place // quarter, lax.rem(place, quarter)
-    own_group = lax.rem(b, groups)
+
+    lead = quarter // 2
 
     def near_target(i):
         return side * half + lax.rem(place - i + half, half)
 
     def far_target(i):
-        return (1 - side) * half + (i // quarter) * quarter + lax.rem(spot - lax.rem(i, quarter) + quarter, quarter)
+        return (1 - side) * half + lax.rem(i, 2) * quarter + lax.rem(spot - i // 2 + quarter, quarter)
 
     def far_slot(i):
-        return half + lax.rem(step + side + 1, 2) * quarter + lax.rem(i, quarter)
+        turn, ring = i // 2, lax.rem(step + side + 1, 2)
+        first = jnp.where(turn < lead, turn, 2 * turn - lead)
+        second = jnp.where(turn < lead, lead + 2 * turn + 1, quarter + turn)
+        return half + jnp.where(ring == 0, first, second)
 
     def near_source(i):
         return side * half + lax.rem(place + i, half)
 
     def far_source(i):
         far = i - half
-        ring = far // quarter
-        return (1 - side) * half + lax.rem(side + ring, 2) * quarter + lax.rem(spot + lax.rem(far, quarter), quarter)
+        middle = far - lead
+        ring = jnp.where(far < lead, 0, jnp.where(middle < quarter, lax.rem(middle + quarter, 2), 1))
+        turn = jnp.where(
+            far < lead, far, jnp.where(middle < quarter, middle // 2 + (1 - ring) * lead, far - quarter)
+        )
+        return (1 - side) * half + lax.rem(side + ring, 2) * quarter + lax.rem(spot + turn, quarter)
 
     def slot_rows(i):
         return pl.ds(pl.multiple_of(i * cap, cap), cap)
@@ -61,47 +69,53 @@
     for j in range(1, peers):
         pl.semaphore_signal(barrier, inc=1, device_id=(b, lax.rem(h + j, peers)), device_id_type=MESH)
 
-    get_x = pltpu.make_async_copy(x_hbm, pay.at[:, :, pl.ds(0, width)], local_sem.at[0])
-    get_cot = pltpu.make_async_copy(cot_hbm, pay.at[:, :, pl.ds(width, width)], local_sem.at[1])
-    get_x.start()
-    get_cot.start()
-
-    lane = lax.broadcasted_iota(jnp.int32, tag.shape, 1)
-    limit = jnp.zeros(tag.shape, jnp.int32)
-    for g in range(groups):
-        limit = jnp.where(lane // cap == g, counts_ref[0, g] + g * cap, limit)
-    tag[...] = jnp.where(lane < limit, ids_ref[...], tasks).astype(jnp.float32)
-    tags[0, 0] = tag[...]
-
-    get_x.wait()
-    get_cot.wait()
-    own = pltpu.make_async_copy(pay.at[own_group], buf.at[0, pl.ds(0, cap)], local_sem.at[2])
-    own.start()
+    loads = [
+        pltpu.make_async_copy(source, target, local_sem.at[6 + at])
+        for at, (source, target) in enumerate(
+            [(counts_hbm, counts_ref), (gate_hbm, gate_ref), (ids_hbm, ids_ref), (cot_hbm, cots)]
+            + [(x_hbm, pay.at[pl.ds(r * groups, groups), :, pl.ds(0, width)]) for r in range(n // groups)]
+        )
+    ]
+    for load in loads:
+        load.start()
     get_w1 = pltpu.make_async_copy(w1_hbm.at[0], w1, local_sem.at[3])
     get_w2 = pltpu.make_async_copy(w2_hbm.at[0], w2, local_sem.at[4])
     get_w1.start()
     get_w2.start()
+    for load in loads[:4]:
+        load.wait()
+    slots = groups * cap
+    lanes = lax.broadcasted_iota(jnp.int32, (slots, slots), 1)
+    places = lax.broadcasted_iota(jnp.int32, (slots, slots), 0)
+    ids = jnp.broadcast_to(ids_ref[...].astype(jnp.float32), (slots, slots))
+    tag[...] = jnp.broadcast_to(
+        jnp.sum(jnp.where(lanes == places, ids, 0.0), axis=1, keepdims=True), tag.shape
+    )
+    order = lax.broadcasted_iota(jnp.int32, (cap, 1), 0)
+
+    @pl.loop(0, groups)
+    def _(g):
+        known = tag[slot_rows(g), :][:, 0:1]
+        live = order < counts_ref[0, g]
+        cot_rows = cots[g].astype(jnp.float32)
+        for r in range(n // groups):
+            gate = jnp.zeros((cap, 1), jnp.float32)
+            for t in range(tasks):
+                gate = jnp.where(known == float(t), gate_ref[t, r * groups + g], gate)
+            gate = jnp.where(live, gate, 0.0)
+            pay[r * groups + g, :, pl.ds(width, width)] = (gate * cot_rows).astype(jnp.bfloat16)
+
+    for load in loads[4:]:
+        load.wait()
+    own = pltpu.make_async_copy(pay.at[b], buf.at[0, pl.ds(0, cap)], local_sem.at[2])
+    own.start()
     pl.semaphore_wait(barrier, n - 1 + peers - 1)
 
     def block_out(target, at, slot):
         return pltpu.make_async_remote_copy(
-            src_ref=pay.at[lax.rem(target, groups)], dst_ref=buf.at[0, slot_rows(slot)],
+            src_ref=pay.at[target], dst_ref=buf.at[0, slot_rows(slot)],
             send_sem=send1.at[at], recv_sem=recv1.at[slot],
             device_id=(target, h), device_id_type=MESH,
-        )
-
-    def tag_out(target, at, slot):
-        return pltpu.make_async_remote_copy(
-            src_ref=tag, dst_ref=tags.at[0, slot],
-            send_sem=tag_send.at[at], recv_sem=tag_recv.at[slot],
-            device_id=(target, h), device_id_type=MESH,
-        )
-
-    def tags_on(j):
-        return pltpu.make_async_remote_copy(
-            src_ref=tags.at[0], dst_ref=tags.at[j],
-            send_sem=tag_pass.at[j - 1], recv_sem=tag_take.at[j - 1],
-            device_id=(b, lax.rem(h + j, peers)), device_id_type=MESH,
         )
 
     def forward(i, j):
@@ -127,12 +141,10 @@
 
     @pl.loop(1, half)
     def _(i):
-        tag_out(near_target(i), i, i).start()
         block_out(near_target(i), i, i).start()
 
     @pl.loop(0, half)
     def _(i):
-        tag_out(far_target(i), half + i, far_slot(i)).start()
         block_out(far_target(i), half + i, far_slot(i)).start()
 
     own.wait()
@@ -148,12 +160,6 @@
     def _(i):
         pass_on(i)
 
-    @pl.loop(1, n)
-    def _(i):
-        tag_out(near_target(0), i, i).wait_recv()
-
-    for j in range(1, peers):
-        tags_on(j).start()
     get_w1.wait()
     get_w2.wait()
 
@@ -161,16 +167,7 @@
         first, total = slot * cap, count * cap
         rows = pl.ds(first, total)
         flat = pl.ds(j * plane + first, total)
-        known = tags[j, pl.ds(slot, count)]
-        gates = jnp.zeros_like(known)
-        for t in range(tasks):
-            gates = gates + jnp.where(known == float(t), gate_ref[t, b], 0.0)
-        spread = jnp.broadcast_to(gates, (count, cap, groups * cap))
-        lanes = lax.broadcasted_iota(jnp.int32, spread.shape, 2)
-        places = lax.broadcasted_iota(jnp.int32, spread.shape, 1) + own_group * cap
-        gate = jnp.sum(jnp.where(lanes == places, spread, 0.0), axis=2, keepdims=True).reshape(total, 1)
-        cot_rows = buf[j, rows, pl.ds(width, width)].astype(jnp.float32)
-        sc[flat, :] = (gate * cot_rows).astype(jnp.bfloat16)
+        sc[flat, :] = buf[j, rows, pl.ds(width, width)]
         xh[flat, :] = buf[j, rows, pl.ds(pl.multiple_of(h * width_part, width_part), width_part)]
 
         def hidden_tile(q, keep):
@@ -183,7 +180,7 @@
             if keep:
                 act[flat, pl.ds(pl.multiple_of(q * tile, tile), tile)] = (pre * sig).astype(jnp.bfloat16)
             cot = lax.dot_general(
-                sc[flat, :], w2[columns, :], (((1,), (1,)), ((), ())), preferred_element_type=jnp.float32
+                buf[j, rows, pl.ds(width, width)], w2[columns, :], (((1,), (1,)), ((), ())), preferred_element_type=jnp.float32
             )
             pc[flat, columns] = (cot * (sig * (1.0 + pre * (1.0 - sig)))).astype(jnp.bfloat16)
             hook(q)
@@ -229,8 +226,6 @@
             homeward(i, far_source(i)).start()
 
     for j in range(1, peers):
-        tags_on(j).wait_recv()
-
         @pl.loop(0, n)
         def _(i):
             forward(i, j).wait_recv()
@@ -242,12 +237,9 @@
     @pl.loop(1, n)
     def _(i):
         block_out(near_target(0), i, i).wait_send()
-        tag_out(near_target(0), i, i).wait_send()
         homeward(i, b).wait_send()
 
     for j in range(1, peers):
-        tags_on(j).wait_send()
-
         @pl.loop(0, n)
         def _(i):
             forward(i, j).wait_send()
@@ -266,7 +258,6 @@
     rows = peers * n * cap
     bf16 = jnp.bfloat16
     hbm = pl.BlockSpec(memory_space=pltpu.HBM)
-    smem = pl.BlockSpec(memory_space=pltpu.SMEM)
     vmem = pl.BlockSpec(memory_space=pltpu.VMEM)
     dma = pltpu.SemaphoreType.DMA
     xh, sc, act, pc, home = pl.pallas_call(
@@ -278,28 +269,33 @@
             pltpu.VMEM((rows, hidden), bf16),
             pltpu.VMEM((n, cap, width), bf16),
         ),
-        in_specs=[smem, smem, vmem, hbm, hbm, hbm, hbm],
+        in_specs=[hbm] * 7,
         out_specs=(vmem,) * 5,
         scratch_shapes=[
-            pltpu.VMEM((groups, cap, 2 * width), bf16),
-            pltpu.VMEM((1, slots), jnp.float32),
+            pltpu.SMEM(group_counts.shape, jnp.int32),
+            pltpu.SMEM(task_gate.shape, jnp.float32),
+            pltpu.VMEM((1, slots), jnp.int32),
+            pltpu.VMEM((groups, cap, width), bf16),
+            pltpu.VMEM((slots, slots), jnp.float32),
+            pltpu.VMEM((n, cap, 2 * width), bf16),
             pltpu.VMEM((peers, n * cap, 2 * width), bf16),
-            pltpu.VMEM((peers, n, 1, slots), jnp.float32),
             pltpu.VMEM((width, hidden), bf16),
             pltpu.VMEM((hidden, width), bf16),
             pltpu.VMEM((n * cap, width), bf16),
             dma((n,)), dma((n,)), dma((peers - 1, n)), dma((peers - 1, n)), dma((n,)), dma((n,)),
-            dma((n,)), dma((n,)), dma((peers - 1,)), dma((peers - 1,)), dma((6,)),
+            dma((10 + n // groups,)),
         ],
         compiler_params=pltpu.CompilerParams(
             collective_id=0, has_side_effects=True, vmem_limit_bytes=VMEM_BYTES
         ),
     )(
-        group_counts, task_gate, task_ids.reshape(1, slots),
         *(
             pltpu.with_memory_space_constraint(array, pltpu.HBM)
-            for array in (inputs.reshape(groups, cap, width), cotangent.reshape(groups, cap, width), w_in, w_out)
-        ),
+            for array in (
+                group_counts, task_gate, task_ids.reshape(1, slots), inputs.reshape(groups, cap, width),
+                cotangent.reshape(groups, cap, width), w_in, w_out,
+            )
+        )
     )
     turned = (((0,), (0,)), ((), ()))
     first = lax.dot_general(xh, pc, turned, preferred_element_type=jnp.float32) * grad_scale

time: 63 us -> 54.2 us (0.86)
  Pallas kernels: 52.7 us -> 46 us
  local copies, waits for them, and re-layouts: 1.98 us -> 0 us
    pallas_call x1, Pallas kernels: 52.7 us -> 46 us  [on_device(): pl.pallas_call(functools.partial(exchange_kernel, n, peers, groups, cap,...]
    unnamed x6 -> x0, local copies, waits for them, and re-layouts: 1.98 us -> none
where the time goes in v3:
time: 54.2 us; the launch traced here: 54.1 us
  Pallas kernels  46 us (85%)
  matrix products  6.59 us (12%)
  other arithmetic  0.88 us (2%)
  between operations  0.64 us (1%)
    pallas_call x1, Pallas kernels, on_device(): pl.pallas_call(functools.partial(exchange_kernel, n, peers, groups, cap,...  46 us
    dot_general x1, matrix products, on_device(): lax.dot_general(act, sc, turned, preferred_element_type=jnp.float32)  3.3 us
    dot_general x1, matrix products, on_device(): lax.dot_general(xh, pc, turned, preferred_element_type=jnp.float32)  3.29 us

profile of v3, /device:TPU:0, one launch (start us, length us, event | category | flops | bytes accessed | tf_op | source)
XLA Modules:
  0.0 54.1 jit_solution(3353816524361089762)
XLA Ops:
  0.6 46.0 %shard_map.94 = (bf16[512,512]{1,0:T(8,128)(2,1)S(1)}, bf16[512,1024]{1,0:T(8,128)(2,1)S(1)}, bf16[512,1024]{1,0:T(8,128)(2,1)S(1)}, bf16[512,2048]{1,0:T(8,128)(2,1)S(1)}, bf16[16,16,1024]{2,1,0:T(8,128)(2,1)S(1)}) custom-call(s32[1,8]{1,0:T(1,128)} %counts_hbm.1, f32[4,16]{1,0:T(4,128)} %gate_hbm.1, s32[1,128]{1,0:T(1,128)} %bitcast.18, ...), custom_call_target="tpu_custom_call" | custom-call | tf_op jit(solution)/shard_map/pallas_call | solution.py:263
  46.6 0.9 %convert_reduce_fusion = f32[128,1024]{1,0:T(8,128)} fusion(bf16[2,128,1024]{2,1,0:T(8,128)(2,1)S(1)} %bitcast.15), kind=kLoop, calls=%fused_computation.2 | loop fusion | flops 393216 | bytes 1048576 | tf_op jit(solution)/shard_map/reduce_sum | solution.py:304
  47.5 3.3 %multiply_bitcast_fusion.1 = f32[1,512,2048]{2,1,0:T(8,128)} fusion(bf16[512,512]{1,0:T(8,128)(2,1)S(1)} %get-tuple-element.9, bf16[512,2048]{1,0:T(8,128)(2,1)S(1)} %get-tuple-element.10), kind=kOutput, calls=%fused_computation.1 | convolution fusion | flops 1074790400 | bytes 6815744 | tf_op jit(solution)/shard_map/dot_general | solution.py:301
  50.8 3.3 %multiply_bitcast_fusion = f32[1,1024,1024]{2,1,0:T(8,128)} fusion(bf16[512,1024]{1,0:T(8,128)(2,1)S(1)} %get-tuple-element.11, bf16[512,1024]{1,0:T(8,128)(2,1)S(1)} %get-tuple-element.12), kind=kOutput, calls=%fused_computation | convolution fusion | flops 1074790400 | bytes 6291456 | tf_op jit(solution)/shard_map/dot_general | solution.py:302

commit v4 on v3

--- a/solution.py
+++ b/solution.py
@@ -31,8 +31,6 @@
     side, place = b // half, lax.rem(b, half)
     step, spot = place // quarter, lax.rem(place, quarter)
 
-    lead = quarter // 2
-
     def near_target(i):
         return side * half + lax.rem(place - i + half, half)
 
@@ -40,22 +38,15 @@
         return (1 - side) * half + lax.rem(i, 2) * quarter + lax.rem(spot - i // 2 + quarter, quarter)
 
     def far_slot(i):
-        turn, ring = i // 2, lax.rem(step + side + 1, 2)
-        first = jnp.where(turn < lead, turn, 2 * turn - lead)
-        second = jnp.where(turn < lead, lead + 2 * turn + 1, quarter + turn)
-        return half + jnp.where(ring == 0, first, second)
+        return half + lax.rem(step + side + 1, 2) * quarter + i // 2
 
     def near_source(i):
         return side * half + lax.rem(place + i, half)
 
     def far_source(i):
         far = i - half
-        middle = far - lead
-        ring = jnp.where(far < lead, 0, jnp.where(middle < quarter, lax.rem(middle + quarter, 2), 1))
-        turn = jnp.where(
-            far < lead, far, jnp.where(middle < quarter, middle // 2 + (1 - ring) * lead, far - quarter)
-        )
-        return (1 - side) * half + lax.rem(side + ring, 2) * quarter + lax.rem(spot + turn, quarter)
+        ring = far // quarter
+        return (1 - side) * half + lax.rem(side + ring, 2) * quarter + lax.rem(spot + lax.rem(far, quarter), quarter)
 
     def slot_rows(i):
         return pl.ds(pl.multiple_of(i * cap, cap), cap)
@@ -67,7 +58,11 @@
         pl.semaphore_signal(barrier, inc=1, device_id=(lax.rem(b + k, n), h), device_id_type=MESH)
 
     for j in range(1, peers):
-        pl.semaphore_signal(barrier, inc=1, device_id=(b, lax.rem(h + j, peers)), device_id_type=MESH)
+        @pl.loop(0, half)
+        def _(i):
+            pl.semaphore_signal(
+                barrier, inc=1, device_id=(near_target(i), lax.rem(h + j, peers)), device_id_type=MESH
+            )
 
     loads = [
         pltpu.make_async_copy(source, target, local_sem.at[6 + at])
@@ -109,7 +104,7 @@
         load.wait()
     own = pltpu.make_async_copy(pay.at[b], buf.at[0, pl.ds(0, cap)], local_sem.at[2])
     own.start()
-    pl.semaphore_wait(barrier, n - 1 + peers - 1)
+    pl.semaphore_wait(barrier, n - 1 + (peers - 1) * half)
 
     def block_out(target, at, slot):
         return pltpu.make_async_remote_copy(
@@ -118,6 +113,14 @@
             device_id=(target, h), device_id_type=MESH,
         )
 
+    def across(i, j):
+        target = near_target(i)
+        return pltpu.make_async_remote_copy(
+            src_ref=pay.at[target], dst_ref=buf.at[j, slot_rows(i)],
+            send_sem=send2.at[j - 1, i], recv_sem=recv2.at[j - 1, i],
+            device_id=(target, lax.rem(h + j, peers)), device_id_type=MESH,
+        )
+
     def forward(i, j):
         return pltpu.make_async_remote_copy(
             src_ref=buf.at[0, slot_rows(i)], dst_ref=buf.at[j, slot_rows(i)],
@@ -139,27 +142,35 @@
             device_id=(source, h), device_id_type=MESH,
         )
 
+    for j in range(1, peers):
+        across(0, j).start()
+
     @pl.loop(1, half)
     def _(i):
         block_out(near_target(i), i, i).start()
+        for j in range(1, peers):
+            across(i, j).start()
 
     @pl.loop(0, half)
     def _(i):
         block_out(far_target(i), half + i, far_slot(i)).start()
-
-    own.wait()
-    for j in range(1, peers):
-        forward(0, j).start()
 
     def pass_on(i):
         block_out(near_target(0), i, i).wait_recv()
         for j in range(1, peers):
             forward(i, j).start()
 
+    early = half + quarter
+
+    @pl.loop(half, early)
+    def _(i):
+        pass_on(i)
+
     @pl.loop(1, half)
     def _(i):
-        pass_on(i)
-
+        block_out(near_target(0), i, i).wait_recv()
+
+    own.wait()
     get_w1.wait()
     get_w2.wait()
 
@@ -204,33 +215,43 @@
             )
             ret[rows, columns] = grad.astype(jnp.bfloat16)
 
-    rows_forward(0, 0, half, lambda q: None)
-    rows_home(0, half)
+    def partner_rows(j, first, count, hook):
+        @pl.loop(first, first + count)
+        def _(i):
+            forward(i, j).wait_recv()
+
+        rows_forward(j, first, count, hook)
+
+    def late_blocks(q):
+        @pl.loop(early + quarter * q // tiles, early + quarter * (q + 1) // tiles)
+        def _(i):
+            pass_on(i)
+
+    rows_forward(0, 0, early, lambda q: None)
+    rows_home(0, early)
     own_home = pltpu.make_async_copy(ret.at[pl.ds(0, cap)], home.at[b], local_sem.at[5])
     own_home.start()
 
+    @pl.loop(half, early)
+    def _(i):
+        homeward(i, far_source(i)).start()
+
     @pl.loop(1, half)
     def _(i):
         homeward(i, near_source(i)).start()
 
-    for first in (half, half + quarter):
-        @pl.loop(first, first + quarter)
-        def _(i):
-            pass_on(i)
-
-        rows_forward(0, first, quarter, lambda q: None)
-        rows_home(first, quarter)
-
-        @pl.loop(first, first + quarter)
-        def _(i):
-            homeward(i, far_source(i)).start()
-
-    for j in range(1, peers):
-        @pl.loop(0, n)
-        def _(i):
-            forward(i, j).wait_recv()
-
-        rows_forward(j, 0, n, lambda q: None)
+    for j in range(1, peers):
+        partner_rows(j, 0, half, late_blocks if j == 1 else lambda q: None)
+
+    rows_forward(0, early, n - early, lambda q: None)
+    rows_home(early, n - early)
+
+    @pl.loop(early, n)
+    def _(i):
+        homeward(i, far_source(i)).start()
+
+    for j in range(1, peers):
+        partner_rows(j, half, n - half, lambda q: None)
 
     own_home.wait()
 

time: 54.2 us -> 54.7 us (level)
  no operation moved by 1% of the time
where the time goes in v4:
time: 54.7 us; the launch traced here: 54.5 us
  Pallas kernels  46.4 us (85%)
  matrix products  6.6 us (12%)
  other arithmetic  0.88 us (2%)
  between operations  0.64 us (1%)
    pallas_call x1, Pallas kernels, on_device(): pl.pallas_call(functools.partial(exchange_kernel, n, peers, groups, cap,...  46.4 us
    dot_general x1, matrix products, on_device(): lax.dot_general(act, sc, turned, preferred_element_type=jnp.float32)  3.3 us
    dot_general x1, matrix products, on_device(): lax.dot_general(xh, pc, turned, preferred_element_type=jnp.float32)  3.29 us

profile of v4, /device:TPU:0, one launch (start us, length us, event | category | flops | bytes accessed | tf_op | source)
XLA Modules:
  0.0 54.5 jit_solution(13017631981714583419)
XLA Ops:
  0.6 46.4 %shard_map.94 = (bf16[512,512]{1,0:T(8,128)(2,1)S(1)}, bf16[512,1024]{1,0:T(8,128)(2,1)S(1)}, bf16[512,1024]{1,0:T(8,128)(2,1)S(1)}, bf16[512,2048]{1,0:T(8,128)(2,1)S(1)}, bf16[16,16,1024]{2,1,0:T(8,128)(2,1)S(1)}) custom-call(s32[1,8]{1,0:T(1,128)} %counts_hbm.1, f32[4,16]{1,0:T(4,128)} %gate_hbm.1, s32[1,128]{1,0:T(1,128)} %bitcast.18, ...), custom_call_target="tpu_custom_call" | custom-call | tf_op jit(solution)/shard_map/pallas_call | solution.py:284
  47.1 0.9 %convert_reduce_fusion = f32[128,1024]{1,0:T(8,128)} fusion(bf16[2,128,1024]{2,1,0:T(8,128)(2,1)S(1)} %bitcast.15), kind=kLoop, calls=%fused_computation.2 | loop fusion | flops 393216 | bytes 1048576 | tf_op jit(solution)/shard_map/reduce_sum | solution.py:325
  48.0 3.3 %multiply_bitcast_fusion.1 = f32[1,512,2048]{2,1,0:T(8,128)} fusion(bf16[512,512]{1,0:T(8,128)(2,1)S(1)} %get-tuple-element.9, bf16[512,2048]{1,0:T(8,128)(2,1)S(1)} %get-tuple-element.10), kind=kOutput, calls=%fused_computation.1 | convolution fusion | flops 1074790400 | bytes 6815744 | tf_op jit(solution)/shard_map/dot_general | solution.py:322
  51.2 3.3 %multiply_bitcast_fusion = f32[1,1024,1024]{2,1,0:T(8,128)} fusion(bf16[512,1024]{1,0:T(8,128)(2,1)S(1)} %get-tuple-element.11, bf16[512,1024]{1,0:T(8,128)(2,1)S(1)} %get-tuple-element.12), kind=kOutput, calls=%fused_computation | convolution fusion | flops 1074790400 | bytes 6291456 | tf_op jit(solution)/shard_map/dot_general | solution.py:323

commit v5 on v4

--- a/solution.py
+++ b/solution.py
@@ -25,7 +25,7 @@
     half, quarter = n // 2, n // 4
     width_part = width // peers
     hidden_part = hidden // peers
-    tile = 256
+    tile = 512
     tiles = hidden // tile
     part_tiles = hidden_part // tile
     side, place = b // half, lax.rem(b, half)
@@ -222,11 +222,6 @@
 
         rows_forward(j, first, count, hook)
 
-    def late_blocks(q):
-        @pl.loop(early + quarter * q // tiles, early + quarter * (q + 1) // tiles)
-        def _(i):
-            pass_on(i)
-
     rows_forward(0, 0, early, lambda q: None)
     rows_home(0, early)
     own_home = pltpu.make_async_copy(ret.at[pl.ds(0, cap)], home.at[b], local_sem.at[5])
@@ -240,8 +235,9 @@
     def _(i):
         homeward(i, near_source(i)).start()
 
-    for j in range(1, peers):
-        partner_rows(j, 0, half, late_blocks if j == 1 else lambda q: None)
+    @pl.loop(early, n)
+    def _(i):
+        pass_on(i)
 
     rows_forward(0, early, n - early, lambda q: None)
     rows_home(early, n - early)
@@ -251,7 +247,7 @@
         homeward(i, far_source(i)).start()
 
     for j in range(1, peers):
-        partner_rows(j, half, n - half, lambda q: None)
+        partner_rows(j, 0, n, lambda q: None)
 
     own_home.wait()
 

time: 54.7 us -> 52.4 us (0.958)
  Pallas kernels: 46.4 us -> 44.1 us
    pallas_call x1, Pallas kernels: 46.4 us -> 44.1 us  [on_device(): pl.pallas_call(functools.partial(exchange_kernel, n, peers, groups, cap,...]
where the time goes in v5:
time: 52.4 us; the launch traced here: 52.2 us
  Pallas kernels  44.1 us (84%)
  matrix products  6.59 us (13%)
  other arithmetic  0.88 us (2%)
  between operations  0.64 us (1%)
    pallas_call x1, Pallas kernels, on_device(): pl.pallas_call(functools.partial(exchange_kernel, n, peers, groups, cap,...  44.1 us
    dot_general x1, matrix products, on_device(): lax.dot_general(act, sc, turned, preferred_element_type=jnp.float32)  3.3 us
    dot_general x1, matrix products, on_device(): lax.dot_general(xh, pc, turned, preferred_element_type=jnp.float32)  3.29 us

profile of v5, /device:TPU:0, one launch (start us, length us, event | category | flops | bytes accessed | tf_op | source)
XLA Modules:
  0.0 52.2 jit_solution(6992394394227257479)
XLA Ops:
  0.6 44.1 %shard_map.94 = (bf16[512,512]{1,0:T(8,128)(2,1)S(1)}, bf16[512,1024]{1,0:T(8,128)(2,1)S(1)}, bf16[512,1024]{1,0:T(8,128)(2,1)S(1)}, bf16[512,2048]{1,0:T(8,128)(2,1)S(1)}, bf16[16,16,1024]{2,1,0:T(8,128)(2,1)S(1)}) custom-call(s32[1,8]{1,0:T(1,128)} %counts_hbm.1, f32[4,16]{1,0:T(4,128)} %gate_hbm.1, s32[1,128]{1,0:T(1,128)} %bitcast.18, ...), custom_call_target="tpu_custom_call" | custom-call | tf_op jit(solution)/shard_map/pallas_call | solution.py:280
  44.8 0.9 %convert_reduce_fusion = f32[128,1024]{1,0:T(8,128)} fusion(bf16[2,128,1024]{2,1,0:T(8,128)(2,1)S(1)} %bitcast.15), kind=kLoop, calls=%fused_computation.2 | loop fusion | flops 393216 | bytes 1048576 | tf_op jit(solution)/shard_map/reduce_sum | solution.py:321
  45.7 3.3 %multiply_bitcast_fusion.1 = f32[1,512,2048]{2,1,0:T(8,128)} fusion(bf16[512,512]{1,0:T(8,128)(2,1)S(1)} %get-tuple-element.9, bf16[512,2048]{1,0:T(8,128)(2,1)S(1)} %get-tuple-element.10), kind=kOutput, calls=%fused_computation.1 | convolution fusion | flops 1074790400 | bytes 6815744 | tf_op jit(solution)/shard_map/dot_general | solution.py:318
  48.9 3.3 %multiply_bitcast_fusion = f32[1,1024,1024]{2,1,0:T(8,128)} fusion(bf16[512,1024]{1,0:T(8,128)(2,1)S(1)} %get-tuple-element.11, bf16[512,1024]{1,0:T(8,128)(2,1)S(1)} %get-tuple-element.12), kind=kOutput, calls=%fused_computation | convolution fusion | flops 1074790400 | bytes 6291456 | tf_op jit(solution)/shard_map/dot_general | solution.py:319
